TPU v7x, 128 devices: a whole 4x4x4 slice. The times are simulated.
128 devices in a mesh: slab: 32 (over z, x, core), rhs: 4 (over y).
Axes of the slice: x: 4, y: 4, z: 4, core: 2. Of those that a mesh axis runs over, the one named last changes fastest.
Arguments:
- diag_blocks: float32 [32, 512, 512], P('slab'), may hold values from -1 to 2, as said below
- sub_blocks: float32 [32, 512, 512], P('slab'), may hold values from -1 to 1
- right_side: float32 [256, 16384], P('rhs', 'slab'), may hold values from -6 to 6
- boundary: float32 [512, 256], P(None, 'rhs'), may hold values from -6 to 6
Outputs:
- solution: float32 [256, 16384], P('rhs', 'slab')
Inputs may be any that keep to these rules, and one draw needn't show every extreme that they name: Each diag_blocks tile is lower triangular with diagonal entries from 0.8 to 1.25; each sub_blocks tile is upper triangular (zeros below its diagonal).
All inputs are finite; a program needn't handle non-finite values.
Results may differ from a plain program's by a relative error of at most 0.00021.
Values sent between devices are 32-bit elements; how exact they have to be, the bound alone decides.
No kernel may reach another device: no remote copies, remote signals or barrier semaphores. Data moves between devices by JAX's collectives and lax.ppermute only.
A program may use at most 64 MiB of HBM per device.

v0:
```python
import functools

import jax
import jax.numpy as jnp
from jax import lax
from jax.experimental import pallas as pl
from jax.experimental.pallas import tpu as pltpu
from jax.sharding import Mesh
from jax.sharding import PartitionSpec as P

SLAB = ("z", "x", "c")
ALL = ("z", "x", "c", "y")
F32 = jnp.float32
BF16 = jnp.bfloat16
N = 512
H = 256
Q = 128
R = 64


def split(a):
    hi = a.astype(BF16)
    return hi, (a - hi.astype(F32)).astype(BF16)


def dot(a, b):
    return lax.dot_general(a, b, (((1,), (0,)), ((), ())), preferred_element_type=F32)


def mm(a, b):
    return dot(a[0], b[0]) + (dot(a[0], b[1]) + dot(a[1], b[0]))


def mm_small(a, b):
    ah, al = split(a)
    bh, bl = split(b)
    row = jnp.concatenate([bh, bl], axis=1)
    both = dot(jnp.concatenate([ah, al], axis=1), jnp.concatenate([row, row], axis=0))
    return both[:, :Q] + both[:, Q:]


def local_body(first_ref, diag_ref, sub_ref, right_ref, bound_ref, out_ref):
    row = lax.broadcasted_iota(jnp.int32, (Q, Q), 0)
    col = lax.broadcasted_iota(jnp.int32, (Q, Q), 1)
    eye = row == col

    def block(i, j):
        return diag_ref[0, j * Q:(j + 1) * Q, i * Q:(i + 1) * Q].T

    ups = [block(i, i) for i in range(4)]
    inv = []
    for u in ups:
        d = jnp.where(eye, u, 0.0)
        across = 1.0 / jnp.sum(d, axis=0, keepdims=True)
        down = 1.0 / jnp.sum(d, axis=1, keepdims=True)
        pair = ((row & 1) == 0) & (col == row + 1)
        inv.append(jnp.where(eye, across, jnp.where(pair, -(down * u) * across, 0.0)))
    for level in range(1, 7):
        rb, cb = row >> level, col >> level
        pick = ((rb & 1) == 0) & (cb == rb + 1)
        half = [mm_small(x, jnp.where(pick, u, 0.0)) for x, u in zip(inv, ups)]
        inv = [x - mm_small(h, x) for h, x in zip(half, inv)]
    tiles = []
    for i in (0, 2):
        off = mm_small(mm_small(inv[i], block(i, i + 1)), inv[i + 1])
        zero = jnp.zeros((Q, Q), F32)
        tiles.append(split(jnp.concatenate([
            jnp.concatenate([inv[i], -off], axis=1),
            jnp.concatenate([zero, inv[i + 1]], axis=1)], axis=0)))
    left0 = jnp.concatenate([sub_ref[0, :H, :].T, right_ref[:, :H]], axis=0)
    right0 = jnp.concatenate([sub_ref[0, H:, :].T, right_ref[:, H:]], axis=0)
    left = mm(split(left0), tiles[0])
    cross = split(diag_ref[0, H:, :H].T)
    right = mm(split(right0 - mm(split(left), cross)), tiles[1])
    out_ref[:N, :H] = -left[:N]
    out_ref[:N, H:] = -right[:N]
    out_ref[N:, :H] = left[N:]
    out_ref[N:, H:] = right[N:]

    @pl.when(first_ref[0] == 1)
    def _():
        out_ref[N:, :] += mm(split(bound_ref[...].T), split(out_ref[:N, :]))


def pair_body(core_ref, own_ref, other_ref, hi_ref, lo_ref, vec_ref):
    def go(first, second):
        both = mm(split(first[...]), split(second[:N, :]))
        hi, lo = split(both[:N])
        hi_ref[...] = hi
        lo_ref[...] = lo
        vec_ref[...] = both[N:] + second[N:, :]

    @pl.when(core_ref[0] == 0)
    def _():
        go(own_ref, other_ref)

    @pl.when(core_ref[0] == 1)
    def _():
        go(other_ref, own_ref)


def hop_body(got_ref, had_ref, hi_ref, lo_ref, vec_ref, in_ref, end_ref):
    total = had_ref[...] + got_ref[...]
    in_ref[...] = total
    end_ref[...] = vec_ref[...] + mm(split(total), (hi_ref[...], lo_ref[...]))


def last_body(core_ref, in_ref, end_ref, own_ref, out_ref):
    @pl.when(core_ref[0] == 0)
    def _():
        out_ref[...] = own_ref[N:, :] + mm(split(in_ref[...]), split(own_ref[:N, :]))

    @pl.when(core_ref[0] == 1)
    def _():
        out_ref[...] = end_ref[...]


def kernel(body, outs, name):
    smem = pl.BlockSpec(memory_space=pltpu.SMEM)
    vmem = pl.BlockSpec(memory_space=pltpu.VMEM)

    def call(*args):
        return pl.pallas_call(
            body,
            out_shape=outs,
            in_specs=[smem if a.dtype == jnp.int32 else vmem for a in args],
            out_specs=jax.tree.map(lambda _: vmem, outs),
            name=name,
        )(*args)

    return call


def arr(rows, dtype=F32):
    return jax.ShapeDtypeStruct((rows, N), dtype)


def index(z, x, c, y):
    return ((z * 4 + x) * 2 + c) * 4 + y


def local(diag_blocks, sub_blocks, right_side, boundary):
    core = lax.axis_index("c").astype(jnp.int32).reshape(1)
    first = (lax.axis_index(SLAB) == 0).astype(jnp.int32).reshape(1)
    own = kernel(local_body, arr(N + R), "local")(first, diag_blocks, sub_blocks, right_side, boundary)
    other = lax.ppermute(own, "c", [(0, 1), (1, 0)])
    hi, lo, vec = kernel(pair_body, [arr(N, BF16), arr(N, BF16), arr(R)], "pair")(core, own, other)
    inflow = jnp.zeros((R, N), F32)
    end = vec
    hop = kernel(hop_body, [arr(R), arr(R)], "hop")
    for k in range(15):
        pairs = [(index(k // 4, k % 4, 1, y), index((k + 1) // 4, (k + 1) % 4, 1, y)) for y in range(4)]
        got = lax.ppermute(end, ALL, pairs)
        inflow, end = hop(got, inflow, hi, lo, vec)
    chips = [(z, x, y) for z in range(4) for x in range(4) for y in range(4)]
    down = lax.ppermute(inflow, ALL, [(index(z, x, 1, y), index(z, x, 0, y)) for z, x, y in chips])
    return kernel(last_body, arr(R), "last")(core, down, end, own)


def solution(mesh):
    shape = mesh.devices.reshape(4, 4, 2, 4)
    split_mesh = Mesh(shape, ALL)
    placed = (P(SLAB, None, None), P(SLAB, None, None), P("y", SLAB), P(None, "y"))
    return jax.shard_map(
        local, mesh=split_mesh, in_specs=placed, out_specs=P("y", SLAB), check_vma=False
    )
```

profile of v0, /device:TPU:117, one launch (start us, length us, event | category | flops | bytes accessed | tf_op | source)
XLA Modules:
  0.0 135.5 jit_solution(6668914467964990253)
XLA Ops:
  0.0 1.7 %copy.5.bound_ref = f32[512,64]{1,0:T(8,128)} copy(f32[512,64]{0,1:T(8,128)} %param.7) | data formatting | bytes 262144 | tf_op args[3]
  1.7 6.0 %local.1.own_ref = f32[576,512]{1,0:T(8,128)} custom-call(s32[1]{0:T(128)} %bitcast.1.first_ref, f32[1,512,512]{2,1,0:T(8,128)} %diag_ref.1, f32[1,512,512]{2,1,0:T(8,128)} %sub_ref.1, f32[64,512]{1,0:T(8,128)} %right_ref.1, f32[512,64]{1,0:T(8,128)} %copy.5.bound_ref), custom_call_target="tpu_custom_call" | custom-call | tf_op jit(solution)/shard_map/local/pallas_call | solution.py:123
  7.7 0.7 collective-permute-start
  8.4 2.7 %collective-permute-done.other_ref = f32[576,512]{1,0:T(8,128)S(1)} collective-permute-done((f32[576,512]{1,0:T(8,128)}, f32[576,512]{1,0:T(8,128)S(1)}, u32[]{:S(2)}, u32[]{:S(2)}) %collective-permute-start) | collective-permute-done | bytes 1179680 | tf_op jit(solution)/shard_map/ppermute | solution.py:146
  11.1 1.0 copy-done
  12.1 3.7 %pair.1 = (bf16[512,512]{1,0:T(8,128)(2,1)}, bf16[512,512]{1,0:T(8,128)(2,1)}, f32[64,512]{1,0:T(8,128)}) custom-call(s32[1]{0:T(128)} %bitcast.core_ref, f32[576,512]{1,0:T(8,128)} %local.1.own_ref, f32[576,512]{1,0:T(8,128)} %copy-done), custom_call_target="tpu_custom_call" | custom-call | tf_op jit(solution)/shard_map/pair/pallas_call | solution.py:123
  15.9 0.7 collective-permute-start.1
  16.5 0.7 broadcast_in_dim.3.had_ref
  17.3 2.4 %hop.15 = (f32[64,512]{1,0:T(8,128)}, f32[64,512]{1,0:T(8,128)}) custom-call(f32[64,512]{1,0:T(8,128)} %copy-done.3, f32[64,512]{1,0:T(8,128)} %broadcast_in_dim.3.had_ref, bf16[512,512]{1,0:T(8,128)(2,1)} %get-tuple-element.39.hi_ref, bf16[512,512]{1,0:T(8,128)(2,1)} %get-tuple-element.40.lo_ref, f32[64,512]{1,0:T(8,128)} %get-tuple-element.38.vec_ref), custom_call_target="tpu_custom_call" | custom-call | tf_op jit(solution)/shard_map/hop/pallas_call | solution.py:123
  21.0 2.4 %hop.16 = (f32[64,512]{1,0:T(8,128)}, f32[64,512]{1,0:T(8,128)}) custom-call(f32[64,512]{1,0:T(8,128)} %copy-done.4, f32[64,512]{1,0:T(8,128)} %get-tuple-element.42.had_ref, bf16[512,512]{1,0:T(8,128)(2,1)} %get-tuple-element.39.hi_ref, bf16[512,512]{1,0:T(8,128)(2,1)} %get-tuple-element.40.lo_ref, f32[64,512]{1,0:T(8,128)} %get-tuple-element.38.vec_ref), custom_call_target="tpu_custom_call" | custom-call | tf_op jit(solution)/shard_map/hop/pallas_call | solution.py:123
  24.7 2.4 %hop.17 = (f32[64,512]{1,0:T(8,128)}, f32[64,512]{1,0:T(8,128)}) custom-call(f32[64,512]{1,0:T(8,128)} %copy-done.5, f32[64,512]{1,0:T(8,128)} %get-tuple-element.44.had_ref, bf16[512,512]{1,0:T(8,128)(2,1)} %get-tuple-element.39.hi_ref, bf16[512,512]{1,0:T(8,128)(2,1)} %get-tuple-element.40.lo_ref, f32[64,512]{1,0:T(8,128)} %get-tuple-element.38.vec_ref), custom_call_target="tpu_custom_call" | custom-call | tf_op jit(solution)/shard_map/hop/pallas_call | solution.py:123
  28.4 2.4 %hop.18 = (f32[64,512]{1,0:T(8,128)}, f32[64,512]{1,0:T(8,128)}) custom-call(f32[64,512]{1,0:T(8,128)} %copy-done.6, f32[64,512]{1,0:T(8,128)} %get-tuple-element.46.had_ref, bf16[512,512]{1,0:T(8,128)(2,1)} %get-tuple-element.39.hi_ref, bf16[512,512]{1,0:T(8,128)(2,1)} %get-tuple-element.40.lo_ref, f32[64,512]{1,0:T(8,128)} %get-tuple-element.38.vec_ref), custom_call_target="tpu_custom_call" | custom-call | tf_op jit(solution)/shard_map/hop/pallas_call | solution.py:123
  32.1 2.4 %hop.19 = (f32[64,512]{1,0:T(8,128)}, f32[64,512]{1,0:T(8,128)}) custom-call(f32[64,512]{1,0:T(8,128)} %copy-done.7, f32[64,512]{1,0:T(8,128)} %get-tuple-element.48.had_ref, bf16[512,512]{1,0:T(8,128)(2,1)} %get-tuple-element.39.hi_ref, bf16[512,512]{1,0:T(8,128)(2,1)} %get-tuple-element.40.lo_ref, f32[64,512]{1,0:T(8,128)} %get-tuple-element.38.vec_ref), custom_call_target="tpu_custom_call" | custom-call | tf_op jit(solution)/shard_map/hop/pallas_call | solution.py:123
  35.7 2.4 %hop.20 = (f32[64,512]{1,0:T(8,128)}, f32[64,512]{1,0:T(8,128)}) custom-call(f32[64,512]{1,0:T(8,128)} %copy-done.8, f32[64,512]{1,0:T(8,128)} %get-tuple-element.50.had_ref, bf16[512,512]{1,0:T(8,128)(2,1)} %get-tuple-element.39.hi_ref, bf16[512,512]{1,0:T(8,128)(2,1)} %get-tuple-element.40.lo_ref, f32[64,512]{1,0:T(8,128)} %get-tuple-element.38.vec_ref), custom_call_target="tpu_custom_call" | custom-call | tf_op jit(solution)/shard_map/hop/pallas_call | solution.py:123
  39.4 2.4 %hop.21 = (f32[64,512]{1,0:T(8,128)}, f32[64,512]{1,0:T(8,128)}) custom-call(f32[64,512]{1,0:T(8,128)} %copy-done.9, f32[64,512]{1,0:T(8,128)} %get-tuple-element.52.had_ref, bf16[512,512]{1,0:T(8,128)(2,1)} %get-tuple-element.39.hi_ref, bf16[512,512]{1,0:T(8,128)(2,1)} %get-tuple-element.40.lo_ref, f32[64,512]{1,0:T(8,128)} %get-tuple-element.38.vec_ref), custom_call_target="tpu_custom_call" | custom-call | tf_op jit(solution)/shard_map/hop/pallas_call | solution.py:123
  41.8 0.7 collective-permute-start.8
  43.1 2.4 %hop.22 = (f32[64,512]{1,0:T(8,128)}, f32[64,512]{1,0:T(8,128)}) custom-call(f32[64,512]{1,0:T(8,128)} %copy-done.10, f32[64,512]{1,0:T(8,128)} %get-tuple-element.54.had_ref, bf16[512,512]{1,0:T(8,128)(2,1)} %get-tuple-element.39.hi_ref, bf16[512,512]{1,0:T(8,128)(2,1)} %get-tuple-element.40.lo_ref, f32[64,512]{1,0:T(8,128)} %get-tuple-element.38.vec_ref), custom_call_target="tpu_custom_call" | custom-call | tf_op jit(solution)/shard_map/hop/pallas_call | solution.py:123
  46.8 2.4 %hop.23 = (f32[64,512]{1,0:T(8,128)}, f32[64,512]{1,0:T(8,128)}) custom-call(f32[64,512]{1,0:T(8,128)} %copy-done.11, f32[64,512]{1,0:T(8,128)} %get-tuple-element.56.had_ref, bf16[512,512]{1,0:T(8,128)(2,1)} %get-tuple-element.39.hi_ref, bf16[512,512]{1,0:T(8,128)(2,1)} %get-tuple-element.40.lo_ref, f32[64,512]{1,0:T(8,128)} %get-tuple-element.38.vec_ref), custom_call_target="tpu_custom_call" | custom-call | tf_op jit(solution)/shard_map/hop/pallas_call | solution.py:123
  50.5 2.4 %hop.24 = (f32[64,512]{1,0:T(8,128)}, f32[64,512]{1,0:T(8,128)}) custom-call(f32[64,512]{1,0:T(8,128)} %copy-done.12, f32[64,512]{1,0:T(8,128)} %get-tuple-element.58.had_ref, bf16[512,512]{1,0:T(8,128)(2,1)} %get-tuple-element.39.hi_ref, bf16[512,512]{1,0:T(8,128)(2,1)} %get-tuple-element.40.lo_ref, f32[64,512]{1,0:T(8,128)} %get-tuple-element.38.vec_ref), custom_call_target="tpu_custom_call" | custom-call | tf_op jit(solution)/shard_map/hop/pallas_call | solution.py:123
  54.2 2.4 %hop.25 = (f32[64,512]{1,0:T(8,128)}, f32[64,512]{1,0:T(8,128)}) custom-call(f32[64,512]{1,0:T(8,128)} %copy-done.13, f32[64,512]{1,0:T(8,128)} %get-tuple-element.60.had_ref, bf16[512,512]{1,0:T(8,128)(2,1)} %get-tuple-element.39.hi_ref, bf16[512,512]{1,0:T(8,128)(2,1)} %get-tuple-element.40.lo_ref, f32[64,512]{1,0:T(8,128)} %get-tuple-element.38.vec_ref), custom_call_target="tpu_custom_call" | custom-call | tf_op jit(solution)/shard_map/hop/pallas_call | solution.py:123
  57.9 2.4 %hop.26 = (f32[64,512]{1,0:T(8,128)}, f32[64,512]{1,0:T(8,128)}) custom-call(f32[64,512]{1,0:T(8,128)} %copy-done.14, f32[64,512]{1,0:T(8,128)} %get-tuple-element.62.had_ref, bf16[512,512]{1,0:T(8,128)(2,1)} %get-tuple-element.39.hi_ref, bf16[512,512]{1,0:T(8,128)(2,1)} %get-tuple-element.40.lo_ref, f32[64,512]{1,0:T(8,128)} %get-tuple-element.38.vec_ref), custom_call_target="tpu_custom_call" | custom-call | tf_op jit(solution)/shard_map/hop/pallas_call | solution.py:123
  61.6 2.4 %hop.27 = (f32[64,512]{1,0:T(8,128)}, f32[64,512]{1,0:T(8,128)}) custom-call(f32[64,512]{1,0:T(8,128)} %copy-done.15, f32[64,512]{1,0:T(8,128)} %get-tuple-element.64.had_ref, bf16[512,512]{1,0:T(8,128)(2,1)} %get-tuple-element.39.hi_ref, bf16[512,512]{1,0:T(8,128)(2,1)} %get-tuple-element.40.lo_ref, f32[64,512]{1,0:T(8,128)} %get-tuple-element.38.vec_ref), custom_call_target="tpu_custom_call" | custom-call | tf_op jit(solution)/shard_map/hop/pallas_call | solution.py:123
  64.0 1.3 collective-permute-start.14
  65.3 55.4 %collective-permute-done.14.got_ref = f32[64,512]{1,0:T(8,128)S(1)} collective-permute-done((f32[64,512]{1,0:T(8,128)}, f32[64,512]{1,0:T(8,128)S(1)}, u32[]{:S(2)}, u32[]{:S(2)}) %collective-permute-start.14) | collective-permute-done | bytes 131104 | tf_op jit(solution)/shard_map/ppermute | solution.py:153
  120.7 0.7 copy-done.16
  121.4 2.4 %hop.28 = (f32[64,512]{1,0:T(8,128)}, f32[64,512]{1,0:T(8,128)}) custom-call(f32[64,512]{1,0:T(8,128)} %copy-done.16, f32[64,512]{1,0:T(8,128)} %get-tuple-element.66.had_ref, bf16[512,512]{1,0:T(8,128)(2,1)} %get-tuple-element.39.hi_ref, bf16[512,512]{1,0:T(8,128)(2,1)} %get-tuple-element.40.lo_ref, f32[64,512]{1,0:T(8,128)} %get-tuple-element.38.vec_ref), custom_call_target="tpu_custom_call" | custom-call | tf_op jit(solution)/shard_map/hop/pallas_call | solution.py:123
  123.7 1.3 collective-permute-start.15
  125.0 2.2 %collective-permute-done.15.got_ref = f32[64,512]{1,0:T(8,128)S(1)} collective-permute-done((f32[64,512]{1,0:T(8,128)}, f32[64,512]{1,0:T(8,128)S(1)}, u32[]{:S(2)}, u32[]{:S(2)}) %collective-permute-start.15) | collective-permute-done | bytes 131104 | tf_op jit(solution)/shard_map/ppermute | solution.py:153
  127.9 2.4 %hop.29 = (f32[64,512]{1,0:T(8,128)}, f32[64,512]{1,0:T(8,128)}) custom-call(f32[64,512]{1,0:T(8,128)} %copy-done.2, f32[64,512]{1,0:T(8,128)} %get-tuple-element.68.had_ref, bf16[512,512]{1,0:T(8,128)(2,1)} %get-tuple-element.39.hi_ref, bf16[512,512]{1,0:T(8,128)(2,1)} %get-tuple-element.40.lo_ref, f32[64,512]{1,0:T(8,128)} %get-tuple-element.38.vec_ref), custom_call_target="tpu_custom_call" | custom-call | tf_op jit(solution)/shard_map/hop/pallas_call | solution.py:123
  130.3 1.3 collective-permute-start.16
  131.6 1.2 collective-permute-done.16.in_ref
  133.4 2.1 %last.1 = f32[64,512]{1,0:T(8,128)} custom-call(s32[1]{0:T(128)} %bitcast.core_ref, f32[64,512]{1,0:T(8,128)} %copy-done.1, f32[64,512]{1,0:T(8,128)} %get-tuple-element.70.end_ref, f32[576,512]{1,0:T(8,128)} %local.1.own_ref), custom_call_target="tpu_custom_call" | custom-call | tf_op jit(solution)/shard_map/last/pallas_call | solution.py:123
  (56 shorter events, 16.3 us)
Async XLA Ops:
  7.7 3.4 %collective-permute-start = (f32[576,512]{1,0:T(8,128)}, f32[576,512]{1,0:T(8,128)S(1)}, u32[]{:S(2)}, u32[]{:S(2)}) collective-permute-start(f32[576,512]{1,0:T(8,128)} %local.1.own_ref), channel_id=1, source_target_pairs={{0,4},{4,0},{1,5},{5,1},{2,6},{6,2},{3,7},{7,3},{8,12},{12,8},{9,1... | collective-permute-start | bytes 3538952 | tf_op jit(solution)/shard_map/ppermute | solution.py:146
  11.1 1.0 copy-start
  15.9 0.7 collective-permute-start.1
  16.5 0.7 copy-start.3
  19.6 0.7 collective-permute-start.2
  20.3 0.7 copy-start.4
  23.3 0.7 collective-permute-start.3
  24.0 0.7 copy-start.5
  27.0 0.7 collective-permute-start.4
  27.7 0.7 copy-start.6
  30.7 0.7 collective-permute-start.5
  31.4 0.7 copy-start.7
  34.4 0.7 collective-permute-start.6
  35.1 0.7 copy-start.8
  38.1 0.7 collective-permute-start.7
  38.8 0.7 copy-start.9
  41.8 0.7 collective-permute-start.8
  42.5 0.7 copy-start.10
  45.5 0.7 collective-permute-start.9
  46.2 0.7 copy-start.11
  49.2 0.7 collective-permute-start.10
  49.9 0.7 copy-start.12
  52.9 0.7 collective-permute-start.11
  53.6 0.7 copy-start.13
  56.6 0.7 collective-permute-start.12
  57.3 0.7 copy-start.14
  60.3 0.7 collective-permute-start.13
  64.0 56.7 %collective-permute-start.14 = (f32[64,512]{1,0:T(8,128)}, f32[64,512]{1,0:T(8,128)S(1)}, u32[]{:S(2)}, u32[]{:S(2)}) collective-permute-start(f32[64,512]{1,0:T(8,128)} %get-tuple-element.65), channel_id=1, source_target_pairs={{108,116},{109,117},{110,118},{111,119}} | collective-permute-start | bytes 393224 | tf_op jit(solution)/shard_map/ppermute | solution.py:153
  120.7 0.7 copy-start.16
  123.7 3.5 %collective-permute-start.15 = (f32[64,512]{1,0:T(8,128)}, f32[64,512]{1,0:T(8,128)S(1)}, u32[]{:S(2)}, u32[]{:S(2)}) collective-permute-start(f32[64,512]{1,0:T(8,128)} %get-tuple-element.67), channel_id=1, source_target_pairs={{116,124},{117,125},{118,126},{119,127}} | collective-permute-start | bytes 393224 | tf_op jit(solution)/shard_map/ppermute | solution.py:153
  127.3 0.7 copy-start.2
  130.3 2.5 %collective-permute-start.16 = (f32[64,512]{1,0:T(8,128)}, f32[64,512]{1,0:T(8,128)S(1)}, u32[]{:S(2)}, u32[]{:S(2)}) collective-permute-start(f32[64,512]{1,0:T(8,128)} %get-tuple-element.69), channel_id=1, source_target_pairs={{4,0},{5,1},{6,2},{7,3},{12,8},{13,9},{14,10},{15,11},{20,16},{21,... | collective-permute-start | bytes 393224 | tf_op jit(solution)/shard_map/ppermute | solution.py:156
  (2 other events, 1.3 us)
where the time goes:
time: 137 us; the launch traced here: 135 us
  waiting for transfers between devices  61.6 us (45%)
  Pallas kernels  47.3 us (35%)
  local copies, waits for them, and re-layouts  13.2 us (10%)
  starting transfers between devices  13.1 us (10%)
    ppermute x15, waiting for transfers between devices, local(): got = lax.ppermute(end, ALL, pairs)  57.7 us
    pallas_call x18, Pallas kernels, call(): pl.pallas_call(body, out_shape=outs, in_specs=[smem if a.dtype == jnp.int...  47.3 us
    unnamed x35, local copies, waits for them, and re-layouts  12.5 us
    ppermute x15, starting transfers between devices, local(): got = lax.ppermute(end, ALL, pairs)  11.1 us
  transfers between devices with their start and end apart: 17, of which 4 were waited for; matrix products, arithmetic and copies ran while one was open for 0% of the time, Pallas kernels for 0%

commit v1 on v0

--- a/solution.py
+++ b/solution.py
@@ -39,7 +39,15 @@
     return both[:, :Q] + both[:, Q:]
 
 
-def local_body(first_ref, diag_ref, sub_ref, right_ref, bound_ref, out_ref):
+def local_body(first_ref, diag_hbm, sub_hbm, right_hbm, bound_hbm, out_ref, diag_ref, sub_ref, right_ref, bound_ref, sems):
+    loads = [
+        pltpu.make_async_copy(src, dst, sems.at[i])
+        for i, (src, dst) in enumerate([
+            (diag_hbm, diag_ref), (sub_hbm, sub_ref), (right_hbm, right_ref), (bound_hbm, bound_ref)])
+    ]
+    for load in loads:
+        load.start()
+    loads[0].wait()
     row = lax.broadcasted_iota(jnp.int32, (Q, Q), 0)
     col = lax.broadcasted_iota(jnp.int32, (Q, Q), 1)
     eye = row == col
@@ -67,6 +75,8 @@
         tiles.append(split(jnp.concatenate([
             jnp.concatenate([inv[i], -off], axis=1),
             jnp.concatenate([zero, inv[i + 1]], axis=1)], axis=0)))
+    for load in loads[1:]:
+        load.wait()
     left0 = jnp.concatenate([sub_ref[0, :H, :].T, right_ref[:, :H]], axis=0)
     right0 = jnp.concatenate([sub_ref[0, H:, :].T, right_ref[:, H:]], axis=0)
     left = mm(split(left0), tiles[0])
@@ -79,7 +89,7 @@
 
     @pl.when(first_ref[0] == 1)
     def _():
-        out_ref[N:, :] += mm(split(bound_ref[...].T), split(out_ref[:N, :]))
+        out_ref[N:, :] += mm(split(bound_ref[...]), split(out_ref[:N, :]))
 
 
 def pair_body(core_ref, own_ref, other_ref, hi_ref, lo_ref, vec_ref):
@@ -115,17 +125,22 @@
         out_ref[...] = end_ref[...]
 
 
-def kernel(body, outs, name):
+def kernel(body, outs, name, scratch=()):
     smem = pl.BlockSpec(memory_space=pltpu.SMEM)
     vmem = pl.BlockSpec(memory_space=pltpu.VMEM)
+    data = pl.BlockSpec(memory_space=pltpu.HBM) if scratch else vmem
 
     def call(*args):
+        space = pltpu.HBM if scratch else pltpu.VMEM
+        args = [a if a.dtype == jnp.int32 else pltpu.with_memory_space_constraint(a, space) for a in args]
         return pl.pallas_call(
             body,
-            out_shape=outs,
-            in_specs=[smem if a.dtype == jnp.int32 else vmem for a in args],
+            out_shape=jax.tree.map(lambda o: pltpu.VMEM(o.shape, o.dtype), outs),
+            in_specs=[smem if a.dtype == jnp.int32 else data for a in args],
             out_specs=jax.tree.map(lambda _: vmem, outs),
+            scratch_shapes=scratch,
             name=name,
+            compiler_params=pltpu.CompilerParams(vmem_limit_bytes=16 << 20),
         )(*args)
 
     return call
@@ -142,7 +157,12 @@
 def local(diag_blocks, sub_blocks, right_side, boundary):
     core = lax.axis_index("c").astype(jnp.int32).reshape(1)
     first = (lax.axis_index(SLAB) == 0).astype(jnp.int32).reshape(1)
-    own = kernel(local_body, arr(N + R), "local")(first, diag_blocks, sub_blocks, right_side, boundary)
+    loads = [
+        pltpu.VMEM((1, N, N), F32), pltpu.VMEM((1, N, N), F32), pltpu.VMEM((R, N), F32),
+        pltpu.VMEM((R, N), F32), pltpu.SemaphoreType.DMA((4,)),
+    ]
+    own = kernel(local_body, arr(N + R), "local", loads)(
+        first, diag_blocks, sub_blocks, right_side, boundary.T)
     other = lax.ppermute(own, "c", [(0, 1), (1, 0)])
     hi, lo, vec = kernel(pair_body, [arr(N, BF16), arr(N, BF16), arr(R)], "pair")(core, own, other)
     inflow = jnp.zeros((R, N), F32)

time: 137 us -> 85.4 us (0.62)
  Pallas kernels: 47.3 us -> 11.8 us
  local copies, waits for them, and re-layouts: 13.2 us -> 0.67 us
  waiting for transfers between devices: 61.6 us -> 57.9 us
    pallas_call x18, Pallas kernels: 47.3 us -> 11.8 us  [call(): pl.pallas_call(body, out_shape=jax.tree.map(lambda o: pltpu.VMEM(o.shape,...]
    unnamed x35 -> x1, local copies, waits for them, and re-layouts: 12.5 us -> 0.66 us
    ppermute x15, waiting for transfers between devices: 57.7 us -> 54.4 us  [local(): got = lax.ppermute(end, ALL, pairs)]
where the time goes in v1:
time: 85.4 us; the launch traced here: 84 us
  waiting for transfers between devices  57.9 us (68%)
  starting transfers between devices  13.3 us (16%)
  Pallas kernels  11.8 us (14%)
    ppermute x15, waiting for transfers between devices, local(): got = lax.ppermute(end, ALL, pairs)  54.4 us
    pallas_call x18, Pallas kernels, call(): pl.pallas_call(body, out_shape=jax.tree.map(lambda o: pltpu.VMEM(o.shape,...  11.8 us
    ppermute x15, starting transfers between devices, local(): got = lax.ppermute(end, ALL, pairs)  11.3 us
    ppermute x1, waiting for transfers between devices, local(): other = lax.ppermute(own, 'c', [(0, 1), (1, 0)])  2.47 us
  transfers between devices with their start and end apart: 17, of which 4 were waited for; matrix products, arithmetic and copies ran while one was open for 0% of the time, Pallas kernels for 0%

profile of v1, /device:TPU:117, one launch (start us, length us, event | category | flops | bytes accessed | tf_op | source)
XLA Modules:
  0.0 84.0 jit_solution(9139498132977221925)
XLA Ops:
  0.0 4.8 %local.1.own_ref = f32[576,512]{1,0:T(8,128)S(1)} custom-call(s32[1]{0:T(128)} %bitcast.1.first_ref, f32[1,512,512]{2,1,0:T(8,128)} %diag_hbm.1, f32[1,512,512]{2,1,0:T(8,128)} %sub_hbm.1, f32[64,512]{1,0:T(8,128)} %right_hbm.1, f32[64,512]{1,0:T(8,128)} %bitcast.3), custom_call_target="tpu_custom_call" | custom-call | tf_op jit(solution)/shard_map/local/pallas_call | solution.py:136
  4.8 0.8 collective-permute-start
  5.5 2.5 %collective-permute-done.other_ref = f32[576,512]{1,0:T(8,128)S(1)} collective-permute-done((f32[576,512]{1,0:T(8,128)S(1)}, f32[576,512]{1,0:T(8,128)S(1)}, u32[]{:S(2)}, u32[]{:S(2)}) %collective-permute-start) | collective-permute-done | bytes 1179680 | tf_op jit(solution)/shard_map/ppermute | solution.py:166
  8.0 1.1 %pair.1 = (bf16[512,512]{1,0:T(8,128)(2,1)S(1)}, bf16[512,512]{1,0:T(8,128)(2,1)S(1)}, f32[64,512]{1,0:T(8,128)S(1)}) custom-call(s32[1]{0:T(128)} %bitcast.core_ref, f32[576,512]{1,0:T(8,128)S(1)} %local.1.own_ref, f32[576,512]{1,0:T(8,128)S(1)} %collective-permute-done.other_ref), custom_call_target="tpu_custom_call" | custom-call | tf_op jit(solution)/shard_map/pair/pallas_call | solution.py:136
  9.1 0.7 collective-permute-start.1
  9.8 0.4 hop.15
  10.2 0.7 collective-permute-start.2
  10.9 0.4 hop.16
  11.3 0.7 collective-permute-start.3
  12.0 0.4 hop.17
  12.4 0.7 collective-permute-start.4
  13.1 0.4 hop.18
  13.5 0.7 collective-permute-start.5
  14.6 0.7 collective-permute-start.6
  15.3 0.4 hop.20
  15.7 0.7 collective-permute-start.7
  16.4 0.4 hop.21
  16.8 0.7 collective-permute-start.8
  17.9 0.7 collective-permute-start.9
  18.6 0.4 hop.23
  19.0 0.7 collective-permute-start.10
  20.0 0.7 collective-permute-start.11
  20.7 0.4 hop.25
  21.1 0.7 collective-permute-start.12
  22.2 0.7 collective-permute-start.13
  23.3 1.3 %collective-permute-start.14 = (f32[64,512]{1,0:T(8,128)S(1)}, f32[64,512]{1,0:T(8,128)S(1)}, u32[]{:S(2)}, u32[]{:S(2)}) collective-permute-start(f32[64,512]{1,0:T(8,128)S(1)} %get-tuple-element.65), channel_id=1, source_target_pairs={{108,116},{109,117},{110,118},{111,119}} | collective-permute-start | bytes 393224 | tf_op jit(solution)/shard_map/ppermute | solution.py:173
  24.6 52.5 %collective-permute-done.14.got_ref = f32[64,512]{1,0:T(8,128)S(1)} collective-permute-done((f32[64,512]{1,0:T(8,128)S(1)}, f32[64,512]{1,0:T(8,128)S(1)}, u32[]{:S(2)}, u32[]{:S(2)}) %collective-permute-start.14) | collective-permute-done | bytes 131104 | tf_op jit(solution)/shard_map/ppermute | solution.py:173
  77.5 1.3 %collective-permute-start.15 = (f32[64,512]{1,0:T(8,128)S(1)}, f32[64,512]{1,0:T(8,128)S(1)}, u32[]{:S(2)}, u32[]{:S(2)}) collective-permute-start(f32[64,512]{1,0:T(8,128)S(1)} %get-tuple-element.67), channel_id=1, source_target_pairs={{116,124},{117,125},{118,126},{119,127}} | collective-permute-start | bytes 393224 | tf_op jit(solution)/shard_map/ppermute | solution.py:173
  78.8 1.9 %collective-permute-done.15.got_ref = f32[64,512]{1,0:T(8,128)S(1)} collective-permute-done((f32[64,512]{1,0:T(8,128)S(1)}, f32[64,512]{1,0:T(8,128)S(1)}, u32[]{:S(2)}, u32[]{:S(2)}) %collective-permute-start.15) | collective-permute-done | bytes 131104 | tf_op jit(solution)/shard_map/ppermute | solution.py:173
  81.1 1.3 %collective-permute-start.16 = (f32[64,512]{1,0:T(8,128)S(1)}, f32[64,512]{1,0:T(8,128)S(1)}, u32[]{:S(2)}, u32[]{:S(2)}) collective-permute-start(f32[64,512]{1,0:T(8,128)S(1)} %get-tuple-element.69), channel_id=1, source_target_pairs={{4,0},{5,1},{6,2},{7,3},{12,8},{13,9},{14,10},{15,11},{20,16},{21,... | collective-permute-start | bytes 393224 | tf_op jit(solution)/shard_map/ppermute | solution.py:176
  82.4 1.0 %collective-permute-done.16.in_ref = f32[64,512]{1,0:T(8,128)S(1)} collective-permute-done((f32[64,512]{1,0:T(8,128)S(1)}, f32[64,512]{1,0:T(8,128)S(1)}, u32[]{:S(2)}, u32[]{:S(2)}) %collective-permute-start.16) | collective-permute-done | bytes 131104 | tf_op jit(solution)/shard_map/ppermute | solution.py:176
  83.4 0.7 copy.5
  (22 shorter events, 2.8 us)
Async XLA Ops:
  4.8 3.2 %collective-permute-start = (f32[576,512]{1,0:T(8,128)S(1)}, f32[576,512]{1,0:T(8,128)S(1)}, u32[]{:S(2)}, u32[]{:S(2)}) collective-permute-start(f32[576,512]{1,0:T(8,128)S(1)} %local.1.own_ref), channel_id=1, source_target_pairs={{0,4},{4,0},{1,5},{5,1},{2,6},{6,2},{3,7},{7,3},{8,12},{12,8},{9,1... | collective-permute-start | bytes 3538952 | tf_op jit(solution)/shard_map/ppermute | solution.py:166
  9.1 0.7 collective-permute-start.1
  10.2 0.7 collective-permute-start.2
  11.3 0.7 collective-permute-start.3
  12.4 0.7 collective-permute-start.4
  13.5 0.7 collective-permute-start.5
  14.6 0.7 collective-permute-start.6
  15.7 0.7 collective-permute-start.7
  16.8 0.7 collective-permute-start.8
  17.9 0.7 collective-permute-start.9
  19.0 0.7 collective-permute-start.10
  20.0 0.7 collective-permute-start.11
  21.1 0.7 collective-permute-start.12
  22.2 0.7 collective-permute-start.13
  23.3 53.8 %collective-permute-start.14 = (f32[64,512]{1,0:T(8,128)S(1)}, f32[64,512]{1,0:T(8,128)S(1)}, u32[]{:S(2)}, u32[]{:S(2)}) collective-permute-start(f32[64,512]{1,0:T(8,128)S(1)} %get-tuple-element.65), channel_id=1, source_target_pairs={{108,116},{109,117},{110,118},{111,119}} | collective-permute-start | bytes 393224 | tf_op jit(solution)/shard_map/ppermute | solution.py:173
  77.5 3.2 %collective-permute-start.15 = (f32[64,512]{1,0:T(8,128)S(1)}, f32[64,512]{1,0:T(8,128)S(1)}, u32[]{:S(2)}, u32[]{:S(2)}) collective-permute-start(f32[64,512]{1,0:T(8,128)S(1)} %get-tuple-element.67), channel_id=1, source_target_pairs={{116,124},{117,125},{118,126},{119,127}} | collective-permute-start | bytes 393224 | tf_op jit(solution)/shard_map/ppermute | solution.py:173
  81.1 2.3 %collective-permute-start.16 = (f32[64,512]{1,0:T(8,128)S(1)}, f32[64,512]{1,0:T(8,128)S(1)}, u32[]{:S(2)}, u32[]{:S(2)}) collective-permute-start(f32[64,512]{1,0:T(8,128)S(1)} %get-tuple-element.69), channel_id=1, source_target_pairs={{4,0},{5,1},{6,2},{7,3},{12,8},{13,9},{14,10},{15,11},{20,16},{21,... | collective-permute-start | bytes 393224 | tf_op jit(solution)/shard_map/ppermute | solution.py:176

commit v2 on v1

--- a/solution.py
+++ b/solution.py
@@ -39,7 +39,7 @@
     return both[:, :Q] + both[:, Q:]
 
 
-def local_body(first_ref, diag_hbm, sub_hbm, right_hbm, bound_hbm, out_ref, diag_ref, sub_ref, right_ref, bound_ref, sems):
+def local_body(me_ref, diag_hbm, sub_hbm, right_hbm, bound_hbm, out_ref, diag_ref, sub_ref, right_ref, bound_ref, sems):
     loads = [
         pltpu.make_async_copy(src, dst, sems.at[i])
         for i, (src, dst) in enumerate([
@@ -87,24 +87,29 @@
     out_ref[N:, :H] = left[N:]
     out_ref[N:, H:] = right[N:]
 
-    @pl.when(first_ref[0] == 1)
+    @pl.when(me_ref[0] < 4)
     def _():
         out_ref[N:, :] += mm(split(bound_ref[...]), split(out_ref[:N, :]))
 
 
-def pair_body(core_ref, own_ref, other_ref, hi_ref, lo_ref, vec_ref):
+def core_of(me_ref):
+    return (me_ref[0] >> 2) & 1
+
+
+def pair_body(me_ref, own_ref, other_ref, full_ref, hi_ref, lo_ref, vec_ref):
     def go(first, second):
         both = mm(split(first[...]), split(second[:N, :]))
-        hi, lo = split(both[:N])
-        hi_ref[...] = hi
-        lo_ref[...] = lo
-        vec_ref[...] = both[N:] + second[N:, :]
-
-    @pl.when(core_ref[0] == 0)
+        vec = both[N:] + second[N:, :]
+        hi_ref[...], lo_ref[...] = split(both[:N])
+        full_ref[:N, :] = both[:N]
+        full_ref[N:, :] = vec
+        vec_ref[...] = vec
+
+    @pl.when(core_of(me_ref) == 0)
     def _():
         go(own_ref, other_ref)
 
-    @pl.when(core_ref[0] == 1)
+    @pl.when(core_of(me_ref) == 1)
     def _():
         go(other_ref, own_ref)
 
@@ -115,29 +120,54 @@
     end_ref[...] = vec_ref[...] + mm(split(total), (hi_ref[...], lo_ref[...]))
 
 
-def last_body(core_ref, in_ref, end_ref, own_ref, out_ref):
-    @pl.when(core_ref[0] == 0)
+def join_body(me_ref, before_ref, hi_ref, lo_ref, vec_ref, end_ref, jhi_ref, jlo_ref, jvec_ref):
+    both = mm(split(before_ref[...]), (hi_ref[...], lo_ref[...]))
+    jhi_ref[...], jlo_ref[...] = split(both[:N])
+    jvec_ref[...] = jnp.where(me_ref[0] < 32, end_ref[...], both[N:] + vec_ref[...])
+
+
+def tail_body(me_ref, walked_ref, got_ref, in_ref, before_ref, hi_ref, lo_ref, vec_ref, end_ref, out_ref, last_ref):
+    line = me_ref[0] >> 5
+    odd = (me_ref[0] >> 3) & 1
+
+    @pl.when(line == 0)
+    def _():
+        out_ref[...] = walked_ref[...]
+        last_ref[...] = end_ref[...]
+
+    @pl.when((line > 0) & (odd == 1))
+    def _():
+        out_ref[...] = before_ref[N:, :] + mm(split(in_ref[...]), split(before_ref[:N, :]))
+        last_ref[...] = end_ref[...]
+
+    @pl.when((line > 0) & (odd == 0))
+    def _():
+        out_ref[...] = got_ref[...]
+        last_ref[...] = vec_ref[...] + mm(split(got_ref[...]), (hi_ref[...], lo_ref[...]))
+
+
+def last_body(me_ref, in_ref, end_ref, own_ref, out_ref):
+    @pl.when(core_of(me_ref) == 0)
     def _():
         out_ref[...] = own_ref[N:, :] + mm(split(in_ref[...]), split(own_ref[:N, :]))
 
-    @pl.when(core_ref[0] == 1)
+    @pl.when(core_of(me_ref) == 1)
     def _():
         out_ref[...] = end_ref[...]
 
 
 def kernel(body, outs, name, scratch=()):
     smem = pl.BlockSpec(memory_space=pltpu.SMEM)
-    vmem = pl.BlockSpec(memory_space=pltpu.VMEM)
-    data = pl.BlockSpec(memory_space=pltpu.HBM) if scratch else vmem
+    space = pltpu.HBM if scratch else pltpu.VMEM
+    data = pl.BlockSpec(memory_space=space)
 
     def call(*args):
-        space = pltpu.HBM if scratch else pltpu.VMEM
         args = [a if a.dtype == jnp.int32 else pltpu.with_memory_space_constraint(a, space) for a in args]
         return pl.pallas_call(
             body,
-            out_shape=jax.tree.map(lambda o: pltpu.VMEM(o.shape, o.dtype), outs),
+            out_shape=outs,
             in_specs=[smem if a.dtype == jnp.int32 else data for a in args],
-            out_specs=jax.tree.map(lambda _: vmem, outs),
+            out_specs=jax.tree.map(lambda _: pl.BlockSpec(memory_space=pltpu.VMEM), outs),
             scratch_shapes=scratch,
             name=name,
             compiler_params=pltpu.CompilerParams(vmem_limit_bytes=16 << 20),
@@ -147,34 +177,40 @@
 
 
 def arr(rows, dtype=F32):
-    return jax.ShapeDtypeStruct((rows, N), dtype)
-
-
-def index(z, x, c, y):
-    return ((z * 4 + x) * 2 + c) * 4 + y
+    return pltpu.VMEM((rows, N), dtype)
+
+
+def links(chips):
+    return [(chip_a * 8 + 4 + y, chip_b * 8 + 4 + y) for chip_a, chip_b in chips for y in range(4)]
 
 
 def local(diag_blocks, sub_blocks, right_side, boundary):
-    core = lax.axis_index("c").astype(jnp.int32).reshape(1)
-    first = (lax.axis_index(SLAB) == 0).astype(jnp.int32).reshape(1)
+    me = lax.axis_index(ALL).astype(jnp.int32).reshape(1)
     loads = [
         pltpu.VMEM((1, N, N), F32), pltpu.VMEM((1, N, N), F32), pltpu.VMEM((R, N), F32),
         pltpu.VMEM((R, N), F32), pltpu.SemaphoreType.DMA((4,)),
     ]
     own = kernel(local_body, arr(N + R), "local", loads)(
-        first, diag_blocks, sub_blocks, right_side, boundary.T)
+        me, diag_blocks, sub_blocks, right_side, boundary.T)
     other = lax.ppermute(own, "c", [(0, 1), (1, 0)])
-    hi, lo, vec = kernel(pair_body, [arr(N, BF16), arr(N, BF16), arr(R)], "pair")(core, own, other)
-    inflow = jnp.zeros((R, N), F32)
-    end = vec
+    full, hi, lo, vec = kernel(
+        pair_body, [arr(N + R), arr(N, BF16), arr(N, BF16), arr(R)], "pair")(me, own, other)
+    before = lax.ppermute(full, ALL, links([(k, k + 1) for k in range(4, 16, 2)]))
     hop = kernel(hop_body, [arr(R), arr(R)], "hop")
-    for k in range(15):
-        pairs = [(index(k // 4, k % 4, 1, y), index((k + 1) // 4, (k + 1) % 4, 1, y)) for y in range(4)]
-        got = lax.ppermute(end, ALL, pairs)
-        inflow, end = hop(got, inflow, hi, lo, vec)
-    chips = [(z, x, y) for z in range(4) for x in range(4) for y in range(4)]
-    down = lax.ppermute(inflow, ALL, [(index(z, x, 1, y), index(z, x, 0, y)) for z, x, y in chips])
-    return kernel(last_body, arr(R), "last")(core, down, end, own)
+    walked, end = jnp.zeros((R, N), F32), vec
+    for k in range(3):
+        walked, end = hop(lax.ppermute(end, ALL, links([(k, k + 1)])), walked, hi, lo, vec)
+    step = lax.ppermute(end, ALL, links([(3, 5)]))
+    jhi, jlo, jvec = kernel(join_body, [arr(N, BF16), arr(N, BF16), arr(R)], "join")(
+        me, before, hi, lo, vec, end)
+    inflow, end = hop(step, jnp.zeros((R, N), F32), jhi, jlo, jvec)
+    for k in range(5, 15, 2):
+        inflow, end = hop(lax.ppermute(end, ALL, links([(k, k + 2)])), inflow, jhi, jlo, jvec)
+    got = lax.ppermute(end, ALL, links([(k, k + 1) for k in range(3, 15, 2)]))
+    inflow, end = kernel(tail_body, [arr(R), arr(R)], "tail")(
+        me, walked, got, inflow, before, hi, lo, vec, end)
+    down = lax.ppermute(inflow, "c", [(0, 1), (1, 0)])
+    return kernel(last_body, jax.ShapeDtypeStruct((R, N), F32), "last")(me, down, end, own)
 
 
 def solution(mesh):

time: 85.4 us -> 61.9 us (0.72); the launches traced: 84 us -> 61.7 us
  waiting for transfers between devices: 57.9 us -> 38.8 us
  starting transfers between devices: 13.3 us -> 11 us
    ppermute x16 -> x12, waiting for transfers between devices: 55.4 us -> 36.4 us  [the longest x1 25.9 us: local(): got = lax.ppermute(end, ALL, links([(k, k + 1) for k in range(3, 15, 2)]))]
    ppermute x16 -> x12, starting transfers between devices: 12.6 us -> 10.3 us  [the longest x5 3.34 us: local(): lax.ppermute(end, ALL, links([(k, k + 2)]))]
    pallas_call x18 -> x14, Pallas kernels: 11.8 us -> 11.5 us  [call(): pl.pallas_call(body, out_shape=outs, in_specs=[smem if a.dtype == jnp.int...]
  transfers between devices with their start and end apart: 17 -> 13, of which waited for: 4 -> 4; matrix products, arithmetic and copies ran while one was open for 0% -> 0% of each run, Pallas kernels for 0% -> 4%
where the time goes in v2:
time: 61.9 us; the launch traced here: 61.7 us
  waiting for transfers between devices  38.8 us (63%)
  Pallas kernels  11.5 us (19%)
  starting transfers between devices  11 us (18%)
    ppermute x1, waiting for transfers between devices, local(): got = lax.ppermute(end, ALL, links([(k, k + 1) for k in range(3, 15, 2)]))  25.9 us
    pallas_call x14, Pallas kernels, call(): pl.pallas_call(body, out_shape=outs, in_specs=[smem if a.dtype == jnp.int...  11.5 us
    ppermute x1, waiting for transfers between devices, local(): lax.ppermute(full, ALL, links([(k, k + 1) for k in range(4, 16, 2)]))  9.11 us
    ppermute x5, starting transfers between devices, local(): lax.ppermute(end, ALL, links([(k, k + 2)]))  3.34 us
    ppermute x1, starting transfers between devices, local(): lax.ppermute(full, ALL, links([(k, k + 1) for k in range(4, 16, 2)]))  2.89 us
    ppermute x1, waiting for transfers between devices, local(): other = lax.ppermute(own, 'c', [(0, 1), (1, 0)])  2.47 us
    ppermute x3, starting transfers between devices, local(): lax.ppermute(end, ALL, links([(k, k + 1)]))  2.01 us
    ppermute x1, waiting for transfers between devices, local(): down = lax.ppermute(inflow, 'c', [(0, 1), (1, 0)])  1.33 us
  transfers between devices with their start and end apart: 13, of which 4 were waited for; matrix products, arithmetic and copies ran while one was open for 0% of the time, Pallas kernels for 4%

profile of v2, /device:TPU:117, one launch (start us, length us, event | category | flops | bytes accessed | tf_op | source)
XLA Modules:
  0.0 61.7 jit_solution(8385594181342609746)
XLA Ops:
  0.0 4.8 %local.1.own_ref = f32[576,512]{1,0:T(8,128)S(1)} custom-call(s32[1]{0:T(128)} %bitcast.me_ref, f32[1,512,512]{2,1,0:T(8,128)} %diag_hbm.1, f32[1,512,512]{2,1,0:T(8,128)} %sub_hbm.1, f32[64,512]{1,0:T(8,128)} %right_hbm.1, f32[64,512]{1,0:T(8,128)} %bitcast.2), custom_call_target="tpu_custom_call" | custom-call | tf_op jit(solution)/shard_map/local/pallas_call | solution.py:166
  4.8 0.8 %collective-permute-start = (f32[576,512]{1,0:T(8,128)S(1)}, f32[576,512]{1,0:T(8,128)S(1)}, u32[]{:S(2)}, u32[]{:S(2)}) collective-permute-start(f32[576,512]{1,0:T(8,128)S(1)} %local.1.own_ref), channel_id=1, source_target_pairs={{0,4},{4,0},{1,5},{5,1},{2,6},{6,2},{3,7},{7,3},{8,12},{12,8},{9,1... | collective-permute-start | bytes 3538952 | tf_op jit(solution)/shard_map/ppermute | solution.py:195
  5.5 2.5 %collective-permute-done.other_ref = f32[576,512]{1,0:T(8,128)S(1)} collective-permute-done((f32[576,512]{1,0:T(8,128)S(1)}, f32[576,512]{1,0:T(8,128)S(1)}, u32[]{:S(2)}, u32[]{:S(2)}) %collective-permute-start) | collective-permute-done | bytes 1179680 | tf_op jit(solution)/shard_map/ppermute | solution.py:195
  8.0 1.1 %pair.1 = (f32[576,512]{1,0:T(8,128)S(1)}, bf16[512,512]{1,0:T(8,128)(2,1)S(1)}, bf16[512,512]{1,0:T(8,128)(2,1)S(1)}, f32[64,512]{1,0:T(8,128)S(1)}) custom-call(s32[1]{0:T(128)} %bitcast.me_ref, f32[576,512]{1,0:T(8,128)S(1)} %local.1.own_ref, f32[576,512]{1,0:T(8,128)S(1)} %collective-permute-done.other_ref), custom_call_target="tpu_custom_call" | custom-call | tf_op jit(solution)/shard_map/pair/pallas_call | solution.py:166
  9.1 2.9 %collective-permute-start.5 = (f32[576,512]{1,0:T(8,128)S(1)}, f32[576,512]{1,0:T(8,128)S(1)}, u32[]{:S(2)}, u32[]{:S(2)}) collective-permute-start(f32[576,512]{1,0:T(8,128)S(1)} %get-tuple-element.41), channel_id=1, source_target_pairs={{36,44},{37,45},{38,46},{39,47},{52,60},{53,61},{54,62},{55,63},{6... | collective-permute-start | bytes 3538952 | tf_op jit(solution)/shard_map/ppermute | solution.py:198
  12.0 0.7 %collective-permute-start.1 = (f32[64,512]{1,0:T(8,128)S(1)}, f32[64,512]{1,0:T(8,128)S(1)}, u32[]{:S(2)}, u32[]{:S(2)}) collective-permute-start(f32[64,512]{1,0:T(8,128)S(1)} %get-tuple-element.32.vec_ref), channel_id=1, source_target_pairs={{4,12},{5,13},{6,14},{7,15}} | collective-permute-start | bytes 393224 | tf_op jit(solution)/shard_map/ppermute | solution.py:202
  12.7 0.4 hop.9
  13.1 0.7 %collective-permute-start.2 = (f32[64,512]{1,0:T(8,128)S(1)}, f32[64,512]{1,0:T(8,128)S(1)}, u32[]{:S(2)}, u32[]{:S(2)}) collective-permute-start(f32[64,512]{1,0:T(8,128)S(1)} %get-tuple-element.35), channel_id=1, source_target_pairs={{12,20},{13,21},{14,22},{15,23}} | collective-permute-start | bytes 393224 | tf_op jit(solution)/shard_map/ppermute | solution.py:202
  13.8 0.0 collective-permute-done.2.got_ref
  13.8 0.4 hop.10
  14.2 0.7 %collective-permute-start.3 = (f32[64,512]{1,0:T(8,128)S(1)}, f32[64,512]{1,0:T(8,128)S(1)}, u32[]{:S(2)}, u32[]{:S(2)}) collective-permute-start(f32[64,512]{1,0:T(8,128)S(1)} %get-tuple-element.37), channel_id=1, source_target_pairs={{20,28},{21,29},{22,30},{23,31}} | collective-permute-start | bytes 393224 | tf_op jit(solution)/shard_map/ppermute | solution.py:202
  14.9 0.4 hop.11
  15.3 0.7 %collective-permute-start.4 = (f32[64,512]{1,0:T(8,128)S(1)}, f32[64,512]{1,0:T(8,128)S(1)}, u32[]{:S(2)}, u32[]{:S(2)}) collective-permute-start(f32[64,512]{1,0:T(8,128)S(1)} %get-tuple-element.40.end_ref), channel_id=1, source_target_pairs={{28,44},{29,45},{30,46},{31,47}} | collective-permute-start | bytes 393224 | tf_op jit(solution)/shard_map/ppermute | solution.py:203
  16.0 9.1 %collective-permute-done.5.before_ref = f32[576,512]{1,0:T(8,128)S(1)} collective-permute-done((f32[576,512]{1,0:T(8,128)S(1)}, f32[576,512]{1,0:T(8,128)S(1)}, u32[]{:S(2)}, u32[]{:S(2)}) %collective-permute-start.5) | collective-permute-done | bytes 1179680 | tf_op jit(solution)/shard_map/ppermute | solution.py:198
  25.1 1.1 %join.1 = (bf16[512,512]{1,0:T(8,128)(2,1)S(1)}, bf16[512,512]{1,0:T(8,128)(2,1)S(1)}, f32[64,512]{1,0:T(8,128)S(1)}) custom-call(s32[1]{0:T(128)} %bitcast.me_ref, f32[576,512]{1,0:T(8,128)S(1)} %collective-permute-done.5.before_ref, bf16[512,512]{1,0:T(8,128)(2,1)S(1)} %get-tuple-element.33.hi_ref, bf16[512,512]{1,0:T(8,128)(2,1)S(1)} %get-tuple-element.34.lo_ref, ...), custom_call_target="tpu_custom_call" | custom-call | tf_op jit(solution)/shard_map/join/pallas_call | solution.py:166
  26.2 0.4 hop.12
  26.6 0.7 %collective-permute-start.6 = (f32[64,512]{1,0:T(8,128)S(1)}, f32[64,512]{1,0:T(8,128)S(1)}, u32[]{:S(2)}, u32[]{:S(2)}) collective-permute-start(f32[64,512]{1,0:T(8,128)S(1)} %get-tuple-element.45), channel_id=1, source_target_pairs={{44,60},{45,61},{46,62},{47,63}} | collective-permute-start | bytes 393224 | tf_op jit(solution)/shard_map/ppermute | solution.py:208
  27.3 0.4 hop.13
  27.7 0.7 %collective-permute-start.7 = (f32[64,512]{1,0:T(8,128)S(1)}, f32[64,512]{1,0:T(8,128)S(1)}, u32[]{:S(2)}, u32[]{:S(2)}) collective-permute-start(f32[64,512]{1,0:T(8,128)S(1)} %get-tuple-element.47), channel_id=1, source_target_pairs={{60,76},{61,77},{62,78},{63,79}} | collective-permute-start | bytes 393224 | tf_op jit(solution)/shard_map/ppermute | solution.py:208
  28.4 0.4 hop.14
  28.8 0.7 %collective-permute-start.8 = (f32[64,512]{1,0:T(8,128)S(1)}, f32[64,512]{1,0:T(8,128)S(1)}, u32[]{:S(2)}, u32[]{:S(2)}) collective-permute-start(f32[64,512]{1,0:T(8,128)S(1)} %get-tuple-element.49), channel_id=1, source_target_pairs={{76,92},{77,93},{78,94},{79,95}} | collective-permute-start | bytes 393224 | tf_op jit(solution)/shard_map/ppermute | solution.py:208
  29.5 0.4 hop.15
  29.8 0.7 %collective-permute-start.9 = (f32[64,512]{1,0:T(8,128)S(1)}, f32[64,512]{1,0:T(8,128)S(1)}, u32[]{:S(2)}, u32[]{:S(2)}) collective-permute-start(f32[64,512]{1,0:T(8,128)S(1)} %get-tuple-element.51), channel_id=1, source_target_pairs={{92,108},{93,109},{94,110},{95,111}} | collective-permute-start | bytes 393224 | tf_op jit(solution)/shard_map/ppermute | solution.py:208
  30.5 0.4 hop.16
  30.9 0.7 %collective-permute-start.10 = (f32[64,512]{1,0:T(8,128)S(1)}, f32[64,512]{1,0:T(8,128)S(1)}, u32[]{:S(2)}, u32[]{:S(2)}) collective-permute-start(f32[64,512]{1,0:T(8,128)S(1)} %get-tuple-element.53), channel_id=1, source_target_pairs={{108,124},{109,125},{110,126},{111,127}} | collective-permute-start | bytes 393224 | tf_op jit(solution)/shard_map/ppermute | solution.py:208
  31.6 0.4 hop.17
  32.0 1.3 %collective-permute-start.11 = (f32[64,512]{1,0:T(8,128)S(1)}, f32[64,512]{1,0:T(8,128)S(1)}, u32[]{:S(2)}, u32[]{:S(2)}) collective-permute-start(f32[64,512]{1,0:T(8,128)S(1)} %get-tuple-element.55.end_ref), channel_id=1, source_target_pairs={{28,36},{29,37},{30,38},{31,39},{44,52},{45,53},{46,54},{47,55},{6... | collective-permute-start | bytes 393224 | tf_op jit(solution)/shard_map/ppermute | solution.py:209
  33.3 25.9 %collective-permute-done.11.got_ref = f32[64,512]{1,0:T(8,128)S(1)} collective-permute-done((f32[64,512]{1,0:T(8,128)S(1)}, f32[64,512]{1,0:T(8,128)S(1)}, u32[]{:S(2)}, u32[]{:S(2)}) %collective-permute-start.11) | collective-permute-done | bytes 131104 | tf_op jit(solution)/shard_map/ppermute | solution.py:209
  59.2 0.4 tail.1
  59.6 0.1 collective-permute-start.12
  59.7 1.3 %collective-permute-done.12.in_ref = f32[64,512]{1,0:T(8,128)S(1)} collective-permute-done((f32[64,512]{1,0:T(8,128)S(1)}, f32[64,512]{1,0:T(8,128)S(1)}, u32[]{:S(2)}, u32[]{:S(2)}) %collective-permute-start.12) | collective-permute-done | bytes 131104 | tf_op jit(solution)/shard_map/ppermute | solution.py:212
  61.0 0.7 %last.1 = f32[64,512]{1,0:T(8,128)} custom-call(s32[1]{0:T(128)} %bitcast.me_ref, f32[64,512]{1,0:T(8,128)S(1)} %collective-permute-done.12.in_ref, f32[64,512]{1,0:T(8,128)S(1)} %get-tuple-element.58.end_ref, f32[576,512]{1,0:T(8,128)S(1)} %local.1.own_ref), custom_call_target="tpu_custom_call" | custom-call | tf_op jit(solution)/shard_map/last/pallas_call | solution.py:166
  (9 shorter events, 0.0 us)
Async XLA Ops:
  4.8 3.2 %collective-permute-start = (f32[576,512]{1,0:T(8,128)S(1)}, f32[576,512]{1,0:T(8,128)S(1)}, u32[]{:S(2)}, u32[]{:S(2)}) collective-permute-start(f32[576,512]{1,0:T(8,128)S(1)} %local.1.own_ref), channel_id=1, source_target_pairs={{0,4},{4,0},{1,5},{5,1},{2,6},{6,2},{3,7},{7,3},{8,12},{12,8},{9,1... | collective-permute-start | bytes 3538952 | tf_op jit(solution)/shard_map/ppermute | solution.py:195
  9.1 16.0 %collective-permute-start.5 = (f32[576,512]{1,0:T(8,128)S(1)}, f32[576,512]{1,0:T(8,128)S(1)}, u32[]{:S(2)}, u32[]{:S(2)}) collective-permute-start(f32[576,512]{1,0:T(8,128)S(1)} %get-tuple-element.41), channel_id=1, source_target_pairs={{36,44},{37,45},{38,46},{39,47},{52,60},{53,61},{54,62},{55,63},{6... | collective-permute-start | bytes 3538952 | tf_op jit(solution)/shard_map/ppermute | solution.py:198
  12.0 0.7 %collective-permute-start.1 = (f32[64,512]{1,0:T(8,128)S(1)}, f32[64,512]{1,0:T(8,128)S(1)}, u32[]{:S(2)}, u32[]{:S(2)}) collective-permute-start(f32[64,512]{1,0:T(8,128)S(1)} %get-tuple-element.32.vec_ref), channel_id=1, source_target_pairs={{4,12},{5,13},{6,14},{7,15}} | collective-permute-start | bytes 393224 | tf_op jit(solution)/shard_map/ppermute | solution.py:202
  13.1 0.7 %collective-permute-start.2 = (f32[64,512]{1,0:T(8,128)S(1)}, f32[64,512]{1,0:T(8,128)S(1)}, u32[]{:S(2)}, u32[]{:S(2)}) collective-permute-start(f32[64,512]{1,0:T(8,128)S(1)} %get-tuple-element.35), channel_id=1, source_target_pairs={{12,20},{13,21},{14,22},{15,23}} | collective-permute-start | bytes 393224 | tf_op jit(solution)/shard_map/ppermute | solution.py:202
  14.2 0.7 %collective-permute-start.3 = (f32[64,512]{1,0:T(8,128)S(1)}, f32[64,512]{1,0:T(8,128)S(1)}, u32[]{:S(2)}, u32[]{:S(2)}) collective-permute-start(f32[64,512]{1,0:T(8,128)S(1)} %get-tuple-element.37), channel_id=1, source_target_pairs={{20,28},{21,29},{22,30},{23,31}} | collective-permute-start | bytes 393224 | tf_op jit(solution)/shard_map/ppermute | solution.py:202
  15.3 10.9 %collective-permute-start.4 = (f32[64,512]{1,0:T(8,128)S(1)}, f32[64,512]{1,0:T(8,128)S(1)}, u32[]{:S(2)}, u32[]{:S(2)}) collective-permute-start(f32[64,512]{1,0:T(8,128)S(1)} %get-tuple-element.40.end_ref), channel_id=1, source_target_pairs={{28,44},{29,45},{30,46},{31,47}} | collective-permute-start | bytes 393224 | tf_op jit(solution)/shard_map/ppermute | solution.py:203
  26.6 0.7 %collective-permute-start.6 = (f32[64,512]{1,0:T(8,128)S(1)}, f32[64,512]{1,0:T(8,128)S(1)}, u32[]{:S(2)}, u32[]{:S(2)}) collective-permute-start(f32[64,512]{1,0:T(8,128)S(1)} %get-tuple-element.45), channel_id=1, source_target_pairs={{44,60},{45,61},{46,62},{47,63}} | collective-permute-start | bytes 393224 | tf_op jit(solution)/shard_map/ppermute | solution.py:208
  27.7 0.7 %collective-permute-start.7 = (f32[64,512]{1,0:T(8,128)S(1)}, f32[64,512]{1,0:T(8,128)S(1)}, u32[]{:S(2)}, u32[]{:S(2)}) collective-permute-start(f32[64,512]{1,0:T(8,128)S(1)} %get-tuple-element.47), channel_id=1, source_target_pairs={{60,76},{61,77},{62,78},{63,79}} | collective-permute-start | bytes 393224 | tf_op jit(solution)/shard_map/ppermute | solution.py:208
  28.8 0.7 %collective-permute-start.8 = (f32[64,512]{1,0:T(8,128)S(1)}, f32[64,512]{1,0:T(8,128)S(1)}, u32[]{:S(2)}, u32[]{:S(2)}) collective-permute-start(f32[64,512]{1,0:T(8,128)S(1)} %get-tuple-element.49), channel_id=1, source_target_pairs={{76,92},{77,93},{78,94},{79,95}} | collective-permute-start | bytes 393224 | tf_op jit(solution)/shard_map/ppermute | solution.py:208
  29.8 0.7 %collective-permute-start.9 = (f32[64,512]{1,0:T(8,128)S(1)}, f32[64,512]{1,0:T(8,128)S(1)}, u32[]{:S(2)}, u32[]{:S(2)}) collective-permute-start(f32[64,512]{1,0:T(8,128)S(1)} %get-tuple-element.51), channel_id=1, source_target_pairs={{92,108},{93,109},{94,110},{95,111}} | collective-permute-start | bytes 393224 | tf_op jit(solution)/shard_map/ppermute | solution.py:208
  30.9 0.7 %collective-permute-start.10 = (f32[64,512]{1,0:T(8,128)S(1)}, f32[64,512]{1,0:T(8,128)S(1)}, u32[]{:S(2)}, u32[]{:S(2)}) collective-permute-start(f32[64,512]{1,0:T(8,128)S(1)} %get-tuple-element.53), channel_id=1, source_target_pairs={{108,124},{109,125},{110,126},{111,127}} | collective-permute-start | bytes 393224 | tf_op jit(solution)/shard_map/ppermute | solution.py:208
  32.0 27.2 %collective-permute-start.11 = (f32[64,512]{1,0:T(8,128)S(1)}, f32[64,512]{1,0:T(8,128)S(1)}, u32[]{:S(2)}, u32[]{:S(2)}) collective-permute-start(f32[64,512]{1,0:T(8,128)S(1)} %get-tuple-element.55.end_ref), channel_id=1, source_target_pairs={{28,36},{29,37},{30,38},{31,39},{44,52},{45,53},{46,54},{47,55},{6... | collective-permute-start | bytes 393224 | tf_op jit(solution)/shard_map/ppermute | solution.py:209
  59.6 1.4 %collective-permute-start.12 = (f32[64,512]{1,0:T(8,128)S(1)}, f32[64,512]{1,0:T(8,128)S(1)}, u32[]{:S(2)}, u32[]{:S(2)}) collective-permute-start(f32[64,512]{1,0:T(8,128)S(1)} %get-tuple-element.57), channel_id=1, source_target_pairs={{0,4},{4,0},{1,5},{5,1},{2,6},{6,2},{3,7},{7,3},{8,12},{12,8},{9,1... | collective-permute-start | bytes 393224 | tf_op jit(solution)/shard_map/ppermute | solution.py:212

commit v3 on v2

--- a/solution.py
+++ b/solution.py
@@ -7,6 +7,7 @@
 from jax.experimental.pallas import tpu as pltpu
 from jax.sharding import Mesh
 from jax.sharding import PartitionSpec as P
+
 
 SLAB = ("z", "x", "c")
 ALL = ("z", "x", "c", "y")
@@ -96,7 +97,7 @@
     return (me_ref[0] >> 2) & 1
 
 
-def pair_body(me_ref, own_ref, other_ref, full_ref, hi_ref, lo_ref, vec_ref):
+def pair_body(me_ref, own_ref, other_ref, full_ref, piece_ref, hi_ref, lo_ref, vec_ref):
     def go(first, second):
         both = mm(split(first[...]), split(second[:N, :]))
         vec = both[N:] + second[N:, :]
@@ -113,37 +114,75 @@
     def _():
         go(other_ref, own_ref)
 
-
-def hop_body(got_ref, had_ref, hi_ref, lo_ref, vec_ref, in_ref, end_ref):
-    total = had_ref[...] + got_ref[...]
+    piece_ref[:Q, :] = full_ref[pl.ds((me_ref[0] & 3) * Q, Q), :]
+    piece_ref[Q:, :] = vec_ref[...]
+
+
+def arrived(me_ref, value, news):
+    for ref, chips in news:
+        here = functools.reduce(jnp.logical_or, [(me_ref[0] >> 3) == chip for chip in chips])
+        value = jnp.where(here, ref[...], value)
+    return value
+
+
+def hop_body(chip, me_ref, got_ref, had_ref, hi_ref, lo_ref, vec_ref, in_ref, end_ref):
+    total = arrived(me_ref, had_ref[...], [(got_ref, [chip])])
     in_ref[...] = total
     end_ref[...] = vec_ref[...] + mm(split(total), (hi_ref[...], lo_ref[...]))
 
 
-def join_body(me_ref, before_ref, hi_ref, lo_ref, vec_ref, end_ref, jhi_ref, jlo_ref, jvec_ref):
-    both = mm(split(before_ref[...]), (hi_ref[...], lo_ref[...]))
-    jhi_ref[...], jlo_ref[...] = split(both[:N])
-    jvec_ref[...] = jnp.where(me_ref[0] < 32, end_ref[...], both[N:] + vec_ref[...])
-
-
-def tail_body(me_ref, walked_ref, got_ref, in_ref, before_ref, hi_ref, lo_ref, vec_ref, end_ref, out_ref, last_ref):
+def pick_body(chips, me_ref, *refs):
+    *news, out_ref = refs
+    out_ref[...] = arrived(me_ref, jnp.zeros((R, N), F32), list(zip(news, chips)))
+
+
+def near_body(full_ref, hi_ref, lo_ref, vec_ref):
+    hi_ref[...], lo_ref[...] = split(full_ref[:N, :])
+    vec_ref[...] = full_ref[N:, :]
+
+
+def far_body(me_ref, *refs):
+    quarter_ref, *pieces, hi_ref, lo_ref, vec_ref = refs
+    for s, piece in zip((0, 1, 3, 2), [quarter_ref, *pieces]):
+        rows = pl.ds(((me_ref[0] + s) & 3) * Q, Q)
+        hi_ref[rows, :], lo_ref[rows, :] = split(piece[:Q, :])
+    vec_ref[...] = quarter_ref[Q:, :]
+
+
+def line_body(chips, me_ref, *refs):
+    maps, had_ref, news, (in_ref, end_ref) = refs[:12], refs[12], refs[13:-2], refs[-2:]
+    inflow = arrived(me_ref, had_ref[...], list(zip(news, chips)))
+    in_ref[...] = inflow
+    for x in range(4):
+        @pl.when(((me_ref[0] >> 3) & 3) == x)
+        def _():
+            current = inflow
+            for chip in range(4):
+                hi, lo, vec = maps[3 * ((chip - x) % 4):][:3]
+                current = vec[...] + mm(split(current), (hi[...], lo[...]))
+            end_ref[...] = current
+
+
+def final_body(chips, me_ref, *refs):
+    maps, (walked_ref, walk_end_ref, had_ref) = refs[:12], refs[12:15]
+    news, (in_ref, end_ref) = refs[15:-2], refs[-2:]
     line = me_ref[0] >> 5
-    odd = (me_ref[0] >> 3) & 1
 
     @pl.when(line == 0)
     def _():
-        out_ref[...] = walked_ref[...]
-        last_ref[...] = end_ref[...]
-
-    @pl.when((line > 0) & (odd == 1))
-    def _():
-        out_ref[...] = before_ref[N:, :] + mm(split(in_ref[...]), split(before_ref[:N, :]))
-        last_ref[...] = end_ref[...]
-
-    @pl.when((line > 0) & (odd == 0))
-    def _():
-        out_ref[...] = got_ref[...]
-        last_ref[...] = vec_ref[...] + mm(split(got_ref[...]), (hi_ref[...], lo_ref[...]))
+        in_ref[...] = walked_ref[...]
+        end_ref[...] = walk_end_ref[...]
+
+    for x in range(4):
+        @pl.when((line > 0) & (((me_ref[0] >> 3) & 3) == x))
+        def _():
+            current = arrived(me_ref, had_ref[...], list(zip(news, chips)))
+            for chip in range(x + 1):
+                if chip == x:
+                    in_ref[...] = current
+                hi, lo, vec = maps[3 * ((chip - x) % 4):][:3]
+                current = vec[...] + mm(split(current), (hi[...], lo[...]))
+            end_ref[...] = current
 
 
 def last_body(me_ref, in_ref, end_ref, own_ref, out_ref):
@@ -156,9 +195,8 @@
         out_ref[...] = end_ref[...]
 
 
-def kernel(body, outs, name, scratch=()):
+def kernel(body, outs, scratch=(), space=pltpu.VMEM):
     smem = pl.BlockSpec(memory_space=pltpu.SMEM)
-    space = pltpu.HBM if scratch else pltpu.VMEM
     data = pl.BlockSpec(memory_space=space)
 
     def call(*args):
@@ -169,7 +207,6 @@
             in_specs=[smem if a.dtype == jnp.int32 else data for a in args],
             out_specs=jax.tree.map(lambda _: pl.BlockSpec(memory_space=pltpu.VMEM), outs),
             scratch_shapes=scratch,
-            name=name,
             compiler_params=pltpu.CompilerParams(vmem_limit_bytes=16 << 20),
         )(*args)
 
@@ -180,43 +217,90 @@
     return pltpu.VMEM((rows, N), dtype)
 
 
-def links(chips):
-    return [(chip_a * 8 + 4 + y, chip_b * 8 + 4 + y) for chip_a, chip_b in chips for y in range(4)]
+def device(z, x, core, y):
+    return ((z * 4 + x) * 2 + core) * 4 + y
+
+
+def complete(moves):
+    pairs = dict(moves)
+    taken = set(pairs.values())
+    for source, target in list(pairs.items()):
+        for a, b in ((target, target ^ 4), (target ^ 4, source ^ 4), (source ^ 4, source)):
+            if a not in pairs and b not in taken:
+                pairs[a] = b
+                taken.add(b)
+    for i in range(128):
+        if i not in pairs:
+            pairs[i] = i ^ 4
+            taken.add(i ^ 4)
+    assert len(taken) == 128 and all(a != b for a, b in pairs.items())
+    return sorted(pairs.items())
+
+
+def hops(pairs):
+    return complete([(device(*a, 1, y), device(*b, 1, y)) for a, b in pairs for y in range(4)])
+
+
+LINES = [(z, x, y) for z in range(1, 4) for x in range(4) for y in range(4)]
+
+
+def ring(x_step, y_step):
+    return [(device(z, (x + x_step) % 4, 1, (y + y_step) % 4), device(z, x, 1, y)) for z, x, y in LINES]
+
+
+def full_ring(x_step, y_step):
+    return complete(ring(x_step, y_step) + [(device(z, x, 0, y), device(z % 3 + 1, x, 0, y)) for z, x, y in LINES])
 
 
 def local(diag_blocks, sub_blocks, right_side, boundary):
+    def send(value, pairs):
+        return lax.ppermute(value, ALL, pairs)
+
     me = lax.axis_index(ALL).astype(jnp.int32).reshape(1)
     loads = [
         pltpu.VMEM((1, N, N), F32), pltpu.VMEM((1, N, N), F32), pltpu.VMEM((R, N), F32),
         pltpu.VMEM((R, N), F32), pltpu.SemaphoreType.DMA((4,)),
     ]
-    own = kernel(local_body, arr(N + R), "local", loads)(
+    own = kernel(local_body, arr(N + R), loads, pltpu.HBM)(
         me, diag_blocks, sub_blocks, right_side, boundary.T)
     other = lax.ppermute(own, "c", [(0, 1), (1, 0)])
-    full, hi, lo, vec = kernel(
-        pair_body, [arr(N + R), arr(N, BF16), arr(N, BF16), arr(R)], "pair")(me, own, other)
-    before = lax.ppermute(full, ALL, links([(k, k + 1) for k in range(4, 16, 2)]))
-    hop = kernel(hop_body, [arr(R), arr(R)], "hop")
-    walked, end = jnp.zeros((R, N), F32), vec
-    for k in range(3):
-        walked, end = hop(lax.ppermute(end, ALL, links([(k, k + 1)])), walked, hi, lo, vec)
-    step = lax.ppermute(end, ALL, links([(3, 5)]))
-    jhi, jlo, jvec = kernel(join_body, [arr(N, BF16), arr(N, BF16), arr(R)], "join")(
-        me, before, hi, lo, vec, end)
-    inflow, end = hop(step, jnp.zeros((R, N), F32), jhi, jlo, jvec)
-    for k in range(5, 15, 2):
-        inflow, end = hop(lax.ppermute(end, ALL, links([(k, k + 2)])), inflow, jhi, jlo, jvec)
-    got = lax.ppermute(end, ALL, links([(k, k + 1) for k in range(3, 15, 2)]))
-    inflow, end = kernel(tail_body, [arr(R), arr(R)], "tail")(
-        me, walked, got, inflow, before, hi, lo, vec, end)
+    weights, two = [arr(N, BF16), arr(N, BF16), arr(R)], [arr(R), arr(R)]
+    full, piece, *here = kernel(pair_body, [arr(N + R), arr(Q + R)] + weights)(me, own, other)
+    hi, lo, vec = here
+
+    quarters = [send(piece, full_ring(2, 0))]
+    left = send(full, ring(-1, 0))
+    right = send(full, ring(1, 0))
+    quarters += [send(quarters[0][:Q], full_ring(0, s)) for s in (1, 3, 2)]
+
+    walked, walk_end = jnp.zeros((R, N), F32), vec
+    for x in range(3):
+        got = send(walk_end, hops([((0, x), (0, x + 1))]))
+        hop = kernel(functools.partial(hop_body, x + 1), two)
+        walked, walk_end = hop(me, got, walked, hi, lo, vec)
+    first = send(walk_end, hops([((0, 3), (1, 3))]))
+    second = send(walk_end, hops([((0, 3), (1, 0))]))
+    inflow = kernel(functools.partial(pick_body, [(7,), (4,)]), arr(R))(me, first, second)
+    third = send(inflow, hops([((1, 3), (1, 2)), ((1, 0), (1, 1))]))
+
+    far = kernel(far_body, weights)(me, *quarters)
+    near = kernel(near_body, weights)
+    maps = [*here, *near(right), *far, *near(left)]
+
+    line = kernel(functools.partial(line_body, [(5, 6)]), two)
+    inflow, end = line(me, *maps, inflow, third)
+    fourth = send(end, hops([((1, x), (2, x)) for x in range(4)]))
+    line = kernel(functools.partial(line_body, [(8, 9, 10, 11)]), two)
+    inflow, end = line(me, *maps, inflow, fourth)
+    fifth = send(end, hops([((2, x), (3, x)) for x in range(4)]))
+    inflow, end = kernel(functools.partial(final_body, [(12, 13, 14, 15)]), two)(
+        me, *maps, walked, walk_end, inflow, fifth)
     down = lax.ppermute(inflow, "c", [(0, 1), (1, 0)])
-    return kernel(last_body, jax.ShapeDtypeStruct((R, N), F32), "last")(me, down, end, own)
+    return kernel(last_body, jax.ShapeDtypeStruct((R, N), F32))(me, down, end, own)
 
 
 def solution(mesh):
-    shape = mesh.devices.reshape(4, 4, 2, 4)
-    split_mesh = Mesh(shape, ALL)
+    split_mesh = Mesh(mesh.devices.reshape(4, 4, 2, 4), ALL)
     placed = (P(SLAB, None, None), P(SLAB, None, None), P("y", SLAB), P(None, "y"))
-    return jax.shard_map(
-        local, mesh=split_mesh, in_specs=placed, out_specs=P("y", SLAB), check_vma=False
-    )
+
+    return jax.shard_map(local, mesh=split_mesh, in_specs=placed, out_specs=P("y", SLAB), check_vma=False)

time: 61.9 us -> 60 us (0.969)
  the two profiles are of different devices: /device:TPU:117 before, /device:TPU:97 now
where the time goes in v3:
time: 60 us; the launch traced here: 59.8 us
  waiting for transfers between devices  33.1 us (55%)
  starting transfers between devices  14.7 us (24%)
  Pallas kernels  11.8 us (20%)
    ppermute x14, waiting for transfers between devices, send(): return lax.ppermute(value, ALL, pairs)  29.3 us
    ppermute x14, starting transfers between devices, send(): return lax.ppermute(value, ALL, pairs)  13.8 us
    pallas_call x13, Pallas kernels, call(): pl.pallas_call(body, out_shape=outs, in_specs=[smem if a.dtype == jnp.int...  11.8 us
    ppermute x1, waiting for transfers between devices, local(): other = lax.ppermute(own, 'c', [(0, 1), (1, 0)])  2.47 us
    ppermute x1, waiting for transfers between devices, local(): down = lax.ppermute(inflow, 'c', [(0, 1), (1, 0)])  1.33 us
  transfers between devices with their start and end apart: 16, of which 9 were waited for; matrix products, arithmetic and copies ran while one was open for 0% of the time, Pallas kernels for 3%

profile of v3, /device:TPU:97, one launch (start us, length us, event | category | flops | bytes accessed | tf_op | source)
XLA Modules:
  0.0 59.8 jit_solution(6359522577660984891)
XLA Ops:
  0.0 4.8 %shard_map.46.own_ref = f32[576,512]{1,0:T(8,128)S(1)} custom-call(s32[1]{0:T(128)} %bitcast.me_ref, f32[1,512,512]{2,1,0:T(8,128)} %diag_hbm.1, f32[1,512,512]{2,1,0:T(8,128)} %sub_hbm.1, f32[64,512]{1,0:T(8,128)} %right_hbm.1, f32[64,512]{1,0:T(8,128)} %bitcast.2), custom_call_target="tpu_custom_call" | custom-call | tf_op jit(solution)/shard_map/pallas_call | solution.py:204
  4.8 0.8 %collective-permute-start = (f32[576,512]{1,0:T(8,128)S(1)}, f32[576,512]{1,0:T(8,128)S(1)}, u32[]{:S(2)}, u32[]{:S(2)}) collective-permute-start(f32[576,512]{1,0:T(8,128)S(1)} %shard_map.46.own_ref), channel_id=1, source_target_pairs={{0,4},{4,0},{1,5},{5,1},{2,6},{6,2},{3,7},{7,3},{8,12},{12,8},{9,1... | collective-permute-start | bytes 3538952 | tf_op jit(solution)/shard_map/ppermute | solution.py:266
  5.5 2.5 %collective-permute-done.other_ref = f32[576,512]{1,0:T(8,128)S(1)} collective-permute-done((f32[576,512]{1,0:T(8,128)S(1)}, f32[576,512]{1,0:T(8,128)S(1)}, u32[]{:S(2)}, u32[]{:S(2)}) %collective-permute-start) | collective-permute-done | bytes 1179680 | tf_op jit(solution)/shard_map/ppermute | solution.py:266
  8.0 1.1 %shard_map.47 = (f32[576,512]{1,0:T(8,128)S(1)}, f32[192,512]{1,0:T(8,128)S(1)}, bf16[512,512]{1,0:T(8,128)(2,1)S(1)}, bf16[512,512]{1,0:T(8,128)(2,1)S(1)}, f32[64,512]{1,0:T(8,128)S(1)}) custom-call(s32[1]{0:T(128)} %bitcast.me_ref, f32[576,512]{1,0:T(8,128)S(1)} %shard_map.46.own_ref, f32[576,512]{1,0:T(8,128)S(1)} %collective-permute-done.other_ref), custom_call_target="tpu_custom_call" | custom-call | tf_op jit(solution)/shard_map/pallas_call | solution.py:204
  9.2 4.4 %collective-permute-start.1 = (f32[576,512]{1,0:T(8,128)S(1)}, f32[576,512]{1,0:T(8,128)S(1)}, u32[]{:S(2)}, u32[]{:S(2)}) collective-permute-start(f32[576,512]{1,0:T(8,128)S(1)} %get-tuple-element.34), channel_id=1, source_target_pairs={{44,36},{45,37},{46,38},{47,39},{52,44},{53,45},{54,46},{55,47},{6... | collective-permute-start | bytes 3538952 | tf_op jit(solution)/shard_map/ppermute | solution.py:257
  13.5 1.9 %collective-permute-start.6 = (f32[576,512]{1,0:T(8,128)S(1)}, f32[576,512]{1,0:T(8,128)S(1)}, u32[]{:S(2)}, u32[]{:S(2)}) collective-permute-start(f32[576,512]{1,0:T(8,128)S(1)} %get-tuple-element.34), channel_id=1, source_target_pairs={{60,36},{61,37},{62,38},{63,39},{36,44},{37,45},{38,46},{39,47},{4... | collective-permute-start | bytes 3538952 | tf_op jit(solution)/shard_map/ppermute | solution.py:257
  15.6 1.8 %collective-permute-start.2 = (f32[192,512]{1,0:T(8,128)S(1)}, f32[192,512]{1,0:T(8,128)S(1)}, u32[]{:S(2)}, u32[]{:S(2)}) collective-permute-start(f32[192,512]{1,0:T(8,128)S(1)} %get-tuple-element.38), channel_id=1, source_target_pairs={{0,4},{1,5},{2,6},{3,7},{4,0},{5,1},{6,2},{7,3},{8,12},{9,13},{10,... | collective-permute-start | bytes 1179656 | tf_op jit(solution)/shard_map/ppermute | solution.py:257
  17.4 0.4 shard_map.51
  17.9 1.3 %collective-permute-done.8.got_ref = f32[64,512]{1,0:T(8,128)S(1)} collective-permute-done((f32[64,512]{1,0:T(8,128)S(1)}, f32[64,512]{1,0:T(8,128)S(1)}, u32[]{:S(2)}, u32[]{:S(2)}) %collective-permute-start.8) | collective-permute-done | bytes 131104 | tf_op jit(solution)/shard_map/ppermute | solution.py:257
  19.2 0.4 shard_map.52
  19.6 0.2 collective-permute-start.9
  19.8 1.2 %collective-permute-done.9.got_ref = f32[64,512]{1,0:T(8,128)S(1)} collective-permute-done((f32[64,512]{1,0:T(8,128)S(1)}, f32[64,512]{1,0:T(8,128)S(1)}, u32[]{:S(2)}, u32[]{:S(2)}) %collective-permute-start.9) | collective-permute-done | bytes 131104 | tf_op jit(solution)/shard_map/ppermute | solution.py:257
  21.0 0.4 shard_map.53
  21.4 0.2 collective-permute-start.10
  21.6 0.4 collective-permute-start.11
  22.0 13.1 %collective-permute-done.2.refs_0_ = f32[192,512]{1,0:T(8,128)S(1)} collective-permute-done((f32[192,512]{1,0:T(8,128)S(1)}, f32[192,512]{1,0:T(8,128)S(1)}, u32[]{:S(2)}, u32[]{:S(2)}) %collective-permute-start.2) | collective-permute-done | bytes 393248 | tf_op jit(solution)/shard_map/ppermute | solution.py:257
  35.1 2.8 %collective-permute-start.3 = (f32[128,512]{1,0:T(8,128)S(1)}, f32[128,512]{1,0:T(8,128)S(1)}, u32[]{:S(2)}, u32[]{:S(2)}) collective-permute-start(f32[128,512]{1,0:T(8,128)S(1)} %slice.6), channel_id=1, source_target_pairs={{0,4},{1,5},{2,6},{3,7},{4,0},{5,1},{6,2},{7,3},{8,12},{9,13},{10,... | collective-permute-start | bytes 786440 | tf_op jit(solution)/shard_map/ppermute | solution.py:257
  37.9 1.6 %collective-permute-start.5 = (f32[128,512]{1,0:T(8,128)S(1)}, f32[128,512]{1,0:T(8,128)S(1)}, u32[]{:S(2)}, u32[]{:S(2)}) collective-permute-start(f32[128,512]{1,0:T(8,128)S(1)} %slice.6), channel_id=1, source_target_pairs={{0,4},{1,5},{2,6},{3,7},{4,0},{5,1},{6,2},{7,3},{8,12},{9,13},{10,... | collective-permute-start | bytes 786440 | tf_op jit(solution)/shard_map/ppermute | solution.py:257
  39.6 1.6 %collective-permute-done.3.refs_1_ = f32[128,512]{1,0:T(8,128)S(1)} collective-permute-done((f32[128,512]{1,0:T(8,128)S(1)}, f32[128,512]{1,0:T(8,128)S(1)}, u32[]{:S(2)}, u32[]{:S(2)}) %collective-permute-start.3) | collective-permute-done | bytes 262176 | tf_op jit(solution)/shard_map/ppermute | solution.py:257
  41.2 5.9 %collective-permute-done.4.refs_2_ = f32[128,512]{1,0:T(8,128)S(1)} collective-permute-done((f32[128,512]{1,0:T(8,128)S(1)}, f32[128,512]{1,0:T(8,128)S(1)}, u32[]{:S(2)}, u32[]{:S(2)}) %collective-permute-start.4) | collective-permute-done | bytes 262176 | tf_op jit(solution)/shard_map/ppermute | solution.py:257
  47.1 0.2 shard_map.49
  47.3 0.2 shard_map.48
  47.5 0.2 shard_map.50
  47.7 1.7 %shard_map.55 = (f32[64,512]{1,0:T(8,128)S(1)}, f32[64,512]{1,0:T(8,128)S(1)}) custom-call(s32[1]{0:T(128)} %bitcast.me_ref, bf16[512,512]{1,0:T(8,128)(2,1)S(1)} %get-tuple-element.31.hi_ref.refs_0_, bf16[512,512]{1,0:T(8,128)(2,1)S(1)} %get-tuple-element.32.lo_ref.refs_1_, f32[64,512]{1,0:T(8,128)S(1)} %get-tuple-element.33.vec_ref.refs_2_, ...), custom_call_target="tpu_custom_call" | custom-call | tf_op jit(solution)/shard_map/pallas_call | solution.py:204
  49.4 0.1 collective-permute-start.13
  49.5 1.3 %collective-permute-done.13.refs_13_ = f32[64,512]{1,0:T(8,128)S(1)} collective-permute-done((f32[64,512]{1,0:T(8,128)S(1)}, f32[64,512]{1,0:T(8,128)S(1)}, u32[]{:S(2)}, u32[]{:S(2)}) %collective-permute-start.13) | collective-permute-done | bytes 131104 | tf_op jit(solution)/shard_map/ppermute | solution.py:257
  50.8 1.5 %shard_map.56 = (f32[64,512]{1,0:T(8,128)S(1)}, f32[64,512]{1,0:T(8,128)S(1)}) custom-call(s32[1]{0:T(128)} %bitcast.me_ref, bf16[512,512]{1,0:T(8,128)(2,1)S(1)} %get-tuple-element.31.hi_ref.refs_0_, bf16[512,512]{1,0:T(8,128)(2,1)S(1)} %get-tuple-element.32.lo_ref.refs_1_, f32[64,512]{1,0:T(8,128)S(1)} %get-tuple-element.33.vec_ref.refs_2_, ...), custom_call_target="tpu_custom_call" | custom-call | tf_op jit(solution)/shard_map/pallas_call | solution.py:204
  52.3 0.2 collective-permute-start.14
  52.5 4.8 %collective-permute-done.14.refs_15_ = f32[64,512]{1,0:T(8,128)S(1)} collective-permute-done((f32[64,512]{1,0:T(8,128)S(1)}, f32[64,512]{1,0:T(8,128)S(1)}, u32[]{:S(2)}, u32[]{:S(2)}) %collective-permute-start.14) | collective-permute-done | bytes 131104 | tf_op jit(solution)/shard_map/ppermute | solution.py:257
  57.3 0.4 shard_map.57
  57.8 1.3 %collective-permute-done.15.in_ref = f32[64,512]{1,0:T(8,128)S(1)} collective-permute-done((f32[64,512]{1,0:T(8,128)S(1)}, f32[64,512]{1,0:T(8,128)S(1)}, u32[]{:S(2)}, u32[]{:S(2)}) %collective-permute-start.15) | collective-permute-done | bytes 131104 | tf_op jit(solution)/shard_map/ppermute | solution.py:298
  59.2 0.7 %shard_map.58 = f32[64,512]{1,0:T(8,128)} custom-call(s32[1]{0:T(128)} %bitcast.me_ref, f32[64,512]{1,0:T(8,128)S(1)} %collective-permute-done.15.in_ref, f32[64,512]{1,0:T(8,128)S(1)} %get-tuple-element.56.end_ref, f32[576,512]{1,0:T(8,128)S(1)} %shard_map.46.own_ref), custom_call_target="tpu_custom_call" | custom-call | tf_op jit(solution)/shard_map/pallas_call | solution.py:204
  (15 shorter events, 0.3 us)
Async XLA Ops:
  4.8 3.2 %collective-permute-start = (f32[576,512]{1,0:T(8,128)S(1)}, f32[576,512]{1,0:T(8,128)S(1)}, u32[]{:S(2)}, u32[]{:S(2)}) collective-permute-start(f32[576,512]{1,0:T(8,128)S(1)} %shard_map.46.own_ref), channel_id=1, source_target_pairs={{0,4},{4,0},{1,5},{5,1},{2,6},{6,2},{3,7},{7,3},{8,12},{12,8},{9,1... | collective-permute-start | bytes 3538952 | tf_op jit(solution)/shard_map/ppermute | solution.py:266
  9.2 38.2 %collective-permute-start.1 = (f32[576,512]{1,0:T(8,128)S(1)}, f32[576,512]{1,0:T(8,128)S(1)}, u32[]{:S(2)}, u32[]{:S(2)}) collective-permute-start(f32[576,512]{1,0:T(8,128)S(1)} %get-tuple-element.34), channel_id=1, source_target_pairs={{44,36},{45,37},{46,38},{47,39},{52,44},{53,45},{54,46},{55,47},{6... | collective-permute-start | bytes 3538952 | tf_op jit(solution)/shard_map/ppermute | solution.py:257
  13.5 34.0 %collective-permute-start.6 = (f32[576,512]{1,0:T(8,128)S(1)}, f32[576,512]{1,0:T(8,128)S(1)}, u32[]{:S(2)}, u32[]{:S(2)}) collective-permute-start(f32[576,512]{1,0:T(8,128)S(1)} %get-tuple-element.34), channel_id=1, source_target_pairs={{60,36},{61,37},{62,38},{63,39},{36,44},{37,45},{38,46},{39,47},{4... | collective-permute-start | bytes 3538952 | tf_op jit(solution)/shard_map/ppermute | solution.py:257
  15.5 1.9 %collective-permute-start.7 = (f32[64,512]{1,0:T(8,128)S(1)}, f32[64,512]{1,0:T(8,128)S(1)}, u32[]{:S(2)}, u32[]{:S(2)}) collective-permute-start(f32[64,512]{1,0:T(8,128)S(1)} %get-tuple-element.33.vec_ref.refs_2_), channel_id=1, source_target_pairs={{0,4},{1,5},{2,6},{3,7},{4,12},{5,13},{6,14},{7,15},{8,0},{9,1},{1... | collective-permute-start | bytes 393224 | tf_op jit(solution)/shard_map/ppermute | solution.py:257
  15.6 19.5 %collective-permute-start.2 = (f32[192,512]{1,0:T(8,128)S(1)}, f32[192,512]{1,0:T(8,128)S(1)}, u32[]{:S(2)}, u32[]{:S(2)}) collective-permute-start(f32[192,512]{1,0:T(8,128)S(1)} %get-tuple-element.38), channel_id=1, source_target_pairs={{0,4},{1,5},{2,6},{3,7},{4,0},{5,1},{6,2},{7,3},{8,12},{9,13},{10,... | collective-permute-start | bytes 1179656 | tf_op jit(solution)/shard_map/ppermute | solution.py:257
  17.8 1.4 %collective-permute-start.8 = (f32[64,512]{1,0:T(8,128)S(1)}, f32[64,512]{1,0:T(8,128)S(1)}, u32[]{:S(2)}, u32[]{:S(2)}) collective-permute-start(f32[64,512]{1,0:T(8,128)S(1)} %get-tuple-element.45), channel_id=1, source_target_pairs={{0,4},{1,5},{2,6},{3,7},{4,0},{5,1},{6,2},{7,3},{8,12},{9,13},{10,... | collective-permute-start | bytes 393224 | tf_op jit(solution)/shard_map/ppermute | solution.py:257
  19.6 1.4 %collective-permute-start.9 = (f32[64,512]{1,0:T(8,128)S(1)}, f32[64,512]{1,0:T(8,128)S(1)}, u32[]{:S(2)}, u32[]{:S(2)}) collective-permute-start(f32[64,512]{1,0:T(8,128)S(1)} %get-tuple-element.47), channel_id=1, source_target_pairs={{0,4},{1,5},{2,6},{3,7},{4,0},{5,1},{6,2},{7,3},{8,12},{9,13},{10,... | collective-permute-start | bytes 393224 | tf_op jit(solution)/shard_map/ppermute | solution.py:257
  21.4 16.5 %collective-permute-start.10 = (f32[64,512]{1,0:T(8,128)S(1)}, f32[64,512]{1,0:T(8,128)S(1)}, u32[]{:S(2)}, u32[]{:S(2)}) collective-permute-start(f32[64,512]{1,0:T(8,128)S(1)} %get-tuple-element.50.refs_13_), channel_id=1, source_target_pairs={{0,4},{1,5},{2,6},{3,7},{4,0},{5,1},{6,2},{7,3},{8,12},{9,13},{10,... | collective-permute-start | bytes 393224 | tf_op jit(solution)/shard_map/ppermute | solution.py:257
  21.6 16.3 %collective-permute-start.11 = (f32[64,512]{1,0:T(8,128)S(1)}, f32[64,512]{1,0:T(8,128)S(1)}, u32[]{:S(2)}, u32[]{:S(2)}) collective-permute-start(f32[64,512]{1,0:T(8,128)S(1)} %get-tuple-element.50.refs_13_), channel_id=1, source_target_pairs={{0,4},{1,5},{2,6},{3,7},{4,0},{5,1},{6,2},{7,3},{8,12},{9,13},{10,... | collective-permute-start | bytes 393224 | tf_op jit(solution)/shard_map/ppermute | solution.py:257
  35.1 6.1 %collective-permute-start.3 = (f32[128,512]{1,0:T(8,128)S(1)}, f32[128,512]{1,0:T(8,128)S(1)}, u32[]{:S(2)}, u32[]{:S(2)}) collective-permute-start(f32[128,512]{1,0:T(8,128)S(1)} %slice.6), channel_id=1, source_target_pairs={{0,4},{1,5},{2,6},{3,7},{4,0},{5,1},{6,2},{7,3},{8,12},{9,13},{10,... | collective-permute-start | bytes 786440 | tf_op jit(solution)/shard_map/ppermute | solution.py:257
  37.9 9.2 %collective-permute-start.4 = (f32[128,512]{1,0:T(8,128)S(1)}, f32[128,512]{1,0:T(8,128)S(1)}, u32[]{:S(2)}, u32[]{:S(2)}) collective-permute-start(f32[128,512]{1,0:T(8,128)S(1)} %slice.6), channel_id=1, source_target_pairs={{0,4},{1,5},{2,6},{3,7},{4,0},{5,1},{6,2},{7,3},{8,12},{9,13},{10,... | collective-permute-start | bytes 786440 | tf_op jit(solution)/shard_map/ppermute | solution.py:257
  37.9 9.2 %collective-permute-start.5 = (f32[128,512]{1,0:T(8,128)S(1)}, f32[128,512]{1,0:T(8,128)S(1)}, u32[]{:S(2)}, u32[]{:S(2)}) collective-permute-start(f32[128,512]{1,0:T(8,128)S(1)} %slice.6), channel_id=1, source_target_pairs={{0,4},{1,5},{2,6},{3,7},{4,0},{5,1},{6,2},{7,3},{8,12},{9,13},{10,... | collective-permute-start | bytes 786440 | tf_op jit(solution)/shard_map/ppermute | solution.py:257
  41.2 6.5 %collective-permute-start.12 = (f32[64,512]{1,0:T(8,128)S(1)}, f32[64,512]{1,0:T(8,128)S(1)}, u32[]{:S(2)}, u32[]{:S(2)}) collective-permute-start(f32[64,512]{1,0:T(8,128)S(1)} %shard_map.54.refs_12_), channel_id=1, source_target_pairs={{0,4},{1,5},{2,6},{3,7},{4,0},{5,1},{6,2},{7,3},{8,12},{9,13},{10,... | collective-permute-start | bytes 393224 | tf_op jit(solution)/shard_map/ppermute | solution.py:257
  49.4 1.4 %collective-permute-start.13 = (f32[64,512]{1,0:T(8,128)S(1)}, f32[64,512]{1,0:T(8,128)S(1)}, u32[]{:S(2)}, u32[]{:S(2)}) collective-permute-start(f32[64,512]{1,0:T(8,128)S(1)} %get-tuple-element.52), channel_id=1, source_target_pairs={{0,4},{1,5},{2,6},{3,7},{4,0},{5,1},{6,2},{7,3},{8,12},{9,13},{10,... | collective-permute-start | bytes 393224 | tf_op jit(solution)/shard_map/ppermute | solution.py:257
  52.3 5.0 %collective-permute-start.14 = (f32[64,512]{1,0:T(8,128)S(1)}, f32[64,512]{1,0:T(8,128)S(1)}, u32[]{:S(2)}, u32[]{:S(2)}) collective-permute-start(f32[64,512]{1,0:T(8,128)S(1)} %get-tuple-element.54), channel_id=1, source_target_pairs={{0,4},{1,5},{2,6},{3,7},{4,0},{5,1},{6,2},{7,3},{8,12},{9,13},{10,... | collective-permute-start | bytes 393224 | tf_op jit(solution)/shard_map/ppermute | solution.py:257
  57.7 1.4 %collective-permute-start.15 = (f32[64,512]{1,0:T(8,128)S(1)}, f32[64,512]{1,0:T(8,128)S(1)}, u32[]{:S(2)}, u32[]{:S(2)}) collective-permute-start(f32[64,512]{1,0:T(8,128)S(1)} %get-tuple-element.55), channel_id=1, source_target_pairs={{0,4},{4,0},{1,5},{5,1},{2,6},{6,2},{3,7},{7,3},{8,12},{12,8},{9,1... | collective-permute-start | bytes 393224 | tf_op jit(solution)/shard_map/ppermute | solution.py:298

commit v4 on v3

--- a/solution.py
+++ b/solution.py
@@ -125,10 +125,22 @@
     return value
 
 
-def hop_body(chip, me_ref, got_ref, had_ref, hi_ref, lo_ref, vec_ref, in_ref, end_ref):
-    total = arrived(me_ref, had_ref[...], [(got_ref, [chip])])
-    in_ref[...] = total
-    end_ref[...] = vec_ref[...] + mm(split(total), (hi_ref[...], lo_ref[...]))
+def hop_body(chip, me_ref, got_ref, had_ref, old_ref, hi_ref, lo_ref, vec_ref, in_ref, end_ref):
+    here = (me_ref[0] >> 2) == 2 * chip + 1
+
+    @pl.when(here)
+    def _():
+        in_ref[...] = got_ref[...]
+        end_ref[...] = vec_ref[...] + mm(split(got_ref[...]), (hi_ref[...], lo_ref[...]))
+
+    @pl.when(jnp.logical_not(here))
+    def _():
+        in_ref[...] = had_ref[...]
+        end_ref[...] = old_ref[...]
+
+
+def upper_only(me_ref):
+    return (core_of(me_ref) == 1) & (me_ref[0] >= 32)
 
 
 def pick_body(chips, me_ref, *refs):
@@ -136,25 +148,30 @@
     out_ref[...] = arrived(me_ref, jnp.zeros((R, N), F32), list(zip(news, chips)))
 
 
-def near_body(full_ref, hi_ref, lo_ref, vec_ref):
-    hi_ref[...], lo_ref[...] = split(full_ref[:N, :])
-    vec_ref[...] = full_ref[N:, :]
+def near_body(me_ref, full_ref, hi_ref, lo_ref, vec_ref):
+    @pl.when(upper_only(me_ref))
+    def _():
+        hi_ref[...], lo_ref[...] = split(full_ref[:N, :])
+        vec_ref[...] = full_ref[N:, :]
 
 
 def far_body(me_ref, *refs):
     quarter_ref, *pieces, hi_ref, lo_ref, vec_ref = refs
-    for s, piece in zip((0, 1, 3, 2), [quarter_ref, *pieces]):
-        rows = pl.ds(((me_ref[0] + s) & 3) * Q, Q)
-        hi_ref[rows, :], lo_ref[rows, :] = split(piece[:Q, :])
-    vec_ref[...] = quarter_ref[Q:, :]
-
-
-def line_body(chips, me_ref, *refs):
+
+    @pl.when(upper_only(me_ref))
+    def _():
+        for s, piece in zip((0, 1, 3, 2), [quarter_ref, *pieces]):
+            rows = pl.ds(((me_ref[0] + s) & 3) * Q, Q)
+            hi_ref[rows, :], lo_ref[rows, :] = split(piece[:Q, :])
+        vec_ref[...] = quarter_ref[Q:, :]
+
+
+def line_body(which, chips, me_ref, *refs):
     maps, had_ref, news, (in_ref, end_ref) = refs[:12], refs[12], refs[13:-2], refs[-2:]
     inflow = arrived(me_ref, had_ref[...], list(zip(news, chips)))
     in_ref[...] = inflow
     for x in range(4):
-        @pl.when(((me_ref[0] >> 3) & 3) == x)
+        @pl.when((me_ref[0] >> 2) == 8 * which + 2 * x + 1)
         def _():
             current = inflow
             for chip in range(4):
@@ -174,7 +191,7 @@
         end_ref[...] = walk_end_ref[...]
 
     for x in range(4):
-        @pl.when((line > 0) & (((me_ref[0] >> 3) & 3) == x))
+        @pl.when(upper_only(me_ref) & (((me_ref[0] >> 3) & 3) == x))
         def _():
             current = arrived(me_ref, had_ref[...], list(zip(news, chips)))
             for chip in range(x + 1):
@@ -277,7 +294,7 @@
     for x in range(3):
         got = send(walk_end, hops([((0, x), (0, x + 1))]))
         hop = kernel(functools.partial(hop_body, x + 1), two)
-        walked, walk_end = hop(me, got, walked, hi, lo, vec)
+        walked, walk_end = hop(me, got, walked, walk_end, hi, lo, vec)
     first = send(walk_end, hops([((0, 3), (1, 3))]))
     second = send(walk_end, hops([((0, 3), (1, 0))]))
     inflow = kernel(functools.partial(pick_body, [(7,), (4,)]), arr(R))(me, first, second)
@@ -285,12 +302,12 @@
 
     far = kernel(far_body, weights)(me, *quarters)
     near = kernel(near_body, weights)
-    maps = [*here, *near(right), *far, *near(left)]
-
-    line = kernel(functools.partial(line_body, [(5, 6)]), two)
+    maps = [*here, *near(me, right), *far, *near(me, left)]
+
+    line = kernel(functools.partial(line_body, 1, [(5, 6)]), two)
     inflow, end = line(me, *maps, inflow, third)
     fourth = send(end, hops([((1, x), (2, x)) for x in range(4)]))
-    line = kernel(functools.partial(line_body, [(8, 9, 10, 11)]), two)
+    line = kernel(functools.partial(line_body, 2, [(8, 9, 10, 11)]), two)
     inflow, end = line(me, *maps, inflow, fourth)
     fifth = send(end, hops([((2, x), (3, x)) for x in range(4)]))
     inflow, end = kernel(functools.partial(final_body, [(12, 13, 14, 15)]), two)(

time: 60 us -> 58.6 us (0.977)
  Pallas kernels: 11.8 us -> 7.87 us
  waiting for transfers between devices: 33.1 us -> 35.7 us
    pallas_call x13, Pallas kernels: 11.8 us -> 7.87 us  [call(): pl.pallas_call(body, out_shape=outs, in_specs=[smem if a.dtype == jnp.int...]
    ppermute x14, waiting for transfers between devices: 29.3 us -> 31.9 us  [send(): return lax.ppermute(value, ALL, pairs)]
  transfers between devices with their start and end apart: 16 -> 16, of which waited for: 9 -> 9; matrix products, arithmetic and copies ran while one was open for 0% -> 0% of each run, Pallas kernels for 3% -> 1%
where the time goes in v4:
time: 58.6 us; the launch traced here: 58.4 us
  waiting for transfers between devices  35.7 us (61%)
  starting transfers between devices  14.7 us (25%)
  Pallas kernels  7.87 us (13%)
    ppermute x14, waiting for transfers between devices, send(): return lax.ppermute(value, ALL, pairs)  31.9 us
    ppermute x14, starting transfers between devices, send(): return lax.ppermute(value, ALL, pairs)  13.8 us
    pallas_call x13, Pallas kernels, call(): pl.pallas_call(body, out_shape=outs, in_specs=[smem if a.dtype == jnp.int...  7.87 us
    ppermute x1, waiting for transfers between devices, local(): other = lax.ppermute(own, 'c', [(0, 1), (1, 0)])  2.47 us
    ppermute x1, waiting for transfers between devices, local(): down = lax.ppermute(inflow, 'c', [(0, 1), (1, 0)])  1.33 us
  transfers between devices with their start and end apart: 16, of which 9 were waited for; matrix products, arithmetic and copies ran while one was open for 0% of the time, Pallas kernels for 1%

profile of v4, /device:TPU:97, one launch (start us, length us, event | category | flops | bytes accessed | tf_op | source)
XLA Modules:
  0.0 58.4 jit_solution(15073643543090583800)
XLA Ops:
  0.0 4.8 %shard_map.46.own_ref = f32[576,512]{1,0:T(8,128)S(1)} custom-call(s32[1]{0:T(128)} %bitcast.me_ref, f32[1,512,512]{2,1,0:T(8,128)} %diag_hbm.1, f32[1,512,512]{2,1,0:T(8,128)} %sub_hbm.1, f32[64,512]{1,0:T(8,128)} %right_hbm.1, f32[64,512]{1,0:T(8,128)} %bitcast.2), custom_call_target="tpu_custom_call" | custom-call | tf_op jit(solution)/shard_map/pallas_call | solution.py:221
  4.8 0.8 %collective-permute-start = (f32[576,512]{1,0:T(8,128)S(1)}, f32[576,512]{1,0:T(8,128)S(1)}, u32[]{:S(2)}, u32[]{:S(2)}) collective-permute-start(f32[576,512]{1,0:T(8,128)S(1)} %shard_map.46.own_ref), channel_id=1, source_target_pairs={{0,4},{4,0},{1,5},{5,1},{2,6},{6,2},{3,7},{7,3},{8,12},{12,8},{9,1... | collective-permute-start | bytes 3538952 | tf_op jit(solution)/shard_map/ppermute | solution.py:283
  5.5 2.5 %collective-permute-done.other_ref = f32[576,512]{1,0:T(8,128)S(1)} collective-permute-done((f32[576,512]{1,0:T(8,128)S(1)}, f32[576,512]{1,0:T(8,128)S(1)}, u32[]{:S(2)}, u32[]{:S(2)}) %collective-permute-start) | collective-permute-done | bytes 1179680 | tf_op jit(solution)/shard_map/ppermute | solution.py:283
  8.0 1.1 %shard_map.47 = (f32[576,512]{1,0:T(8,128)S(1)}, f32[192,512]{1,0:T(8,128)S(1)}, bf16[512,512]{1,0:T(8,128)(2,1)S(1)}, bf16[512,512]{1,0:T(8,128)(2,1)S(1)}, f32[64,512]{1,0:T(8,128)S(1)}) custom-call(s32[1]{0:T(128)} %bitcast.me_ref, f32[576,512]{1,0:T(8,128)S(1)} %shard_map.46.own_ref, f32[576,512]{1,0:T(8,128)S(1)} %collective-permute-done.other_ref), custom_call_target="tpu_custom_call" | custom-call | tf_op jit(solution)/shard_map/pallas_call | solution.py:221
  9.2 4.4 %collective-permute-start.1 = (f32[576,512]{1,0:T(8,128)S(1)}, f32[576,512]{1,0:T(8,128)S(1)}, u32[]{:S(2)}, u32[]{:S(2)}) collective-permute-start(f32[576,512]{1,0:T(8,128)S(1)} %get-tuple-element.34), channel_id=1, source_target_pairs={{44,36},{45,37},{46,38},{47,39},{52,44},{53,45},{54,46},{55,47},{6... | collective-permute-start | bytes 3538952 | tf_op jit(solution)/shard_map/ppermute | solution.py:274
  13.5 1.9 %collective-permute-start.6 = (f32[576,512]{1,0:T(8,128)S(1)}, f32[576,512]{1,0:T(8,128)S(1)}, u32[]{:S(2)}, u32[]{:S(2)}) collective-permute-start(f32[576,512]{1,0:T(8,128)S(1)} %get-tuple-element.34), channel_id=1, source_target_pairs={{60,36},{61,37},{62,38},{63,39},{36,44},{37,45},{38,46},{39,47},{4... | collective-permute-start | bytes 3538952 | tf_op jit(solution)/shard_map/ppermute | solution.py:274
  15.5 0.1 collective-permute-start.7
  15.6 1.8 %collective-permute-start.2 = (f32[192,512]{1,0:T(8,128)S(1)}, f32[192,512]{1,0:T(8,128)S(1)}, u32[]{:S(2)}, u32[]{:S(2)}) collective-permute-start(f32[192,512]{1,0:T(8,128)S(1)} %get-tuple-element.38), channel_id=1, source_target_pairs={{0,4},{1,5},{2,6},{3,7},{4,0},{5,1},{6,2},{7,3},{8,12},{9,13},{10,... | collective-permute-start | bytes 1179656 | tf_op jit(solution)/shard_map/ppermute | solution.py:274
  17.4 0.0 collective-permute-done.7.got_ref
  17.4 0.1 collective-permute-start.8
  17.5 1.3 %collective-permute-done.8.got_ref = f32[64,512]{1,0:T(8,128)S(1)} collective-permute-done((f32[64,512]{1,0:T(8,128)S(1)}, f32[64,512]{1,0:T(8,128)S(1)}, u32[]{:S(2)}, u32[]{:S(2)}) %collective-permute-start.8) | collective-permute-done | bytes 131104 | tf_op jit(solution)/shard_map/ppermute | solution.py:274
  18.9 0.2 collective-permute-start.9
  19.1 1.2 %collective-permute-done.9.got_ref = f32[64,512]{1,0:T(8,128)S(1)} collective-permute-done((f32[64,512]{1,0:T(8,128)S(1)}, f32[64,512]{1,0:T(8,128)S(1)}, u32[]{:S(2)}, u32[]{:S(2)}) %collective-permute-start.9) | collective-permute-done | bytes 131104 | tf_op jit(solution)/shard_map/ppermute | solution.py:274
  20.3 0.2 collective-permute-start.10
  20.6 0.4 collective-permute-start.11
  20.9 14.2 %collective-permute-done.2.refs_0_ = f32[192,512]{1,0:T(8,128)S(1)} collective-permute-done((f32[192,512]{1,0:T(8,128)S(1)}, f32[192,512]{1,0:T(8,128)S(1)}, u32[]{:S(2)}, u32[]{:S(2)}) %collective-permute-start.2) | collective-permute-done | bytes 393248 | tf_op jit(solution)/shard_map/ppermute | solution.py:274
  35.1 2.8 %collective-permute-start.3 = (f32[128,512]{1,0:T(8,128)S(1)}, f32[128,512]{1,0:T(8,128)S(1)}, u32[]{:S(2)}, u32[]{:S(2)}) collective-permute-start(f32[128,512]{1,0:T(8,128)S(1)} %slice.6), channel_id=1, source_target_pairs={{0,4},{1,5},{2,6},{3,7},{4,0},{5,1},{6,2},{7,3},{8,12},{9,13},{10,... | collective-permute-start | bytes 786440 | tf_op jit(solution)/shard_map/ppermute | solution.py:274
  37.9 1.6 %collective-permute-start.5 = (f32[128,512]{1,0:T(8,128)S(1)}, f32[128,512]{1,0:T(8,128)S(1)}, u32[]{:S(2)}, u32[]{:S(2)}) collective-permute-start(f32[128,512]{1,0:T(8,128)S(1)} %slice.6), channel_id=1, source_target_pairs={{0,4},{1,5},{2,6},{3,7},{4,0},{5,1},{6,2},{7,3},{8,12},{9,13},{10,... | collective-permute-start | bytes 786440 | tf_op jit(solution)/shard_map/ppermute | solution.py:274
  39.6 1.6 %collective-permute-done.3.refs_1_ = f32[128,512]{1,0:T(8,128)S(1)} collective-permute-done((f32[128,512]{1,0:T(8,128)S(1)}, f32[128,512]{1,0:T(8,128)S(1)}, u32[]{:S(2)}, u32[]{:S(2)}) %collective-permute-start.3) | collective-permute-done | bytes 262176 | tf_op jit(solution)/shard_map/ppermute | solution.py:274
  41.2 5.9 %collective-permute-done.4.refs_2_ = f32[128,512]{1,0:T(8,128)S(1)} collective-permute-done((f32[128,512]{1,0:T(8,128)S(1)}, f32[128,512]{1,0:T(8,128)S(1)}, u32[]{:S(2)}, u32[]{:S(2)}) %collective-permute-start.4) | collective-permute-done | bytes 262176 | tf_op jit(solution)/shard_map/ppermute | solution.py:274
  47.1 0.2 shard_map.49
  47.3 0.2 shard_map.48
  47.5 0.2 shard_map.50
  47.7 0.2 shard_map.55
  47.9 0.1 collective-permute-start.13
  48.0 1.3 %collective-permute-done.13.refs_13_ = f32[64,512]{1,0:T(8,128)S(1)} collective-permute-done((f32[64,512]{1,0:T(8,128)S(1)}, f32[64,512]{1,0:T(8,128)S(1)}, u32[]{:S(2)}, u32[]{:S(2)}) %collective-permute-start.13) | collective-permute-done | bytes 131104 | tf_op jit(solution)/shard_map/ppermute | solution.py:274
  49.4 0.2 collective-permute-start.14
  49.7 6.2 %collective-permute-done.14.refs_15_ = f32[64,512]{1,0:T(8,128)S(1)} collective-permute-done((f32[64,512]{1,0:T(8,128)S(1)}, f32[64,512]{1,0:T(8,128)S(1)}, u32[]{:S(2)}, u32[]{:S(2)}) %collective-permute-start.14) | collective-permute-done | bytes 131104 | tf_op jit(solution)/shard_map/ppermute | solution.py:274
  55.9 0.4 shard_map.57
  56.3 0.1 collective-permute-start.15
  56.4 1.3 %collective-permute-done.15.in_ref = f32[64,512]{1,0:T(8,128)S(1)} collective-permute-done((f32[64,512]{1,0:T(8,128)S(1)}, f32[64,512]{1,0:T(8,128)S(1)}, u32[]{:S(2)}, u32[]{:S(2)}) %collective-permute-start.15) | collective-permute-done | bytes 131104 | tf_op jit(solution)/shard_map/ppermute | solution.py:315
  57.8 0.7 %shard_map.58 = f32[64,512]{1,0:T(8,128)} custom-call(s32[1]{0:T(128)} %bitcast.me_ref, f32[64,512]{1,0:T(8,128)S(1)} %collective-permute-done.15.in_ref, f32[64,512]{1,0:T(8,128)S(1)} %get-tuple-element.56.end_ref, f32[576,512]{1,0:T(8,128)S(1)} %shard_map.46.own_ref), custom_call_target="tpu_custom_call" | custom-call | tf_op jit(solution)/shard_map/pallas_call | solution.py:221
  (15 shorter events, 0.2 us)
Async XLA Ops:
  4.8 3.2 %collective-permute-start = (f32[576,512]{1,0:T(8,128)S(1)}, f32[576,512]{1,0:T(8,128)S(1)}, u32[]{:S(2)}, u32[]{:S(2)}) collective-permute-start(f32[576,512]{1,0:T(8,128)S(1)} %shard_map.46.own_ref), channel_id=1, source_target_pairs={{0,4},{4,0},{1,5},{5,1},{2,6},{6,2},{3,7},{7,3},{8,12},{12,8},{9,1... | collective-permute-start | bytes 3538952 | tf_op jit(solution)/shard_map/ppermute | solution.py:283
  9.2 38.2 %collective-permute-start.1 = (f32[576,512]{1,0:T(8,128)S(1)}, f32[576,512]{1,0:T(8,128)S(1)}, u32[]{:S(2)}, u32[]{:S(2)}) collective-permute-start(f32[576,512]{1,0:T(8,128)S(1)} %get-tuple-element.34), channel_id=1, source_target_pairs={{44,36},{45,37},{46,38},{47,39},{52,44},{53,45},{54,46},{55,47},{6... | collective-permute-start | bytes 3538952 | tf_op jit(solution)/shard_map/ppermute | solution.py:274
  13.5 34.0 %collective-permute-start.6 = (f32[576,512]{1,0:T(8,128)S(1)}, f32[576,512]{1,0:T(8,128)S(1)}, u32[]{:S(2)}, u32[]{:S(2)}) collective-permute-start(f32[576,512]{1,0:T(8,128)S(1)} %get-tuple-element.34), channel_id=1, source_target_pairs={{60,36},{61,37},{62,38},{63,39},{36,44},{37,45},{38,46},{39,47},{4... | collective-permute-start | bytes 3538952 | tf_op jit(solution)/shard_map/ppermute | solution.py:274
  15.5 1.9 %collective-permute-start.7 = (f32[64,512]{1,0:T(8,128)S(1)}, f32[64,512]{1,0:T(8,128)S(1)}, u32[]{:S(2)}, u32[]{:S(2)}) collective-permute-start(f32[64,512]{1,0:T(8,128)S(1)} %get-tuple-element.33.old_ref.vec_ref.refs_2_), channel_id=1, source_target_pairs={{0,4},{1,5},{2,6},{3,7},{4,12},{5,13},{6,14},{7,15},{8,0},{9,1},{1... | collective-permute-start | bytes 393224 | tf_op jit(solution)/shard_map/ppermute | solution.py:274
  15.6 19.5 %collective-permute-start.2 = (f32[192,512]{1,0:T(8,128)S(1)}, f32[192,512]{1,0:T(8,128)S(1)}, u32[]{:S(2)}, u32[]{:S(2)}) collective-permute-start(f32[192,512]{1,0:T(8,128)S(1)} %get-tuple-element.38), channel_id=1, source_target_pairs={{0,4},{1,5},{2,6},{3,7},{4,0},{5,1},{6,2},{7,3},{8,12},{9,13},{10,... | collective-permute-start | bytes 1179656 | tf_op jit(solution)/shard_map/ppermute | solution.py:274
  17.4 1.4 %collective-permute-start.8 = (f32[64,512]{1,0:T(8,128)S(1)}, f32[64,512]{1,0:T(8,128)S(1)}, u32[]{:S(2)}, u32[]{:S(2)}) collective-permute-start(f32[64,512]{1,0:T(8,128)S(1)} %get-tuple-element.45.old_ref), channel_id=1, source_target_pairs={{0,4},{1,5},{2,6},{3,7},{4,0},{5,1},{6,2},{7,3},{8,12},{9,13},{10,... | collective-permute-start | bytes 393224 | tf_op jit(solution)/shard_map/ppermute | solution.py:274
  18.9 1.4 %collective-permute-start.9 = (f32[64,512]{1,0:T(8,128)S(1)}, f32[64,512]{1,0:T(8,128)S(1)}, u32[]{:S(2)}, u32[]{:S(2)}) collective-permute-start(f32[64,512]{1,0:T(8,128)S(1)} %get-tuple-element.47.old_ref), channel_id=1, source_target_pairs={{0,4},{1,5},{2,6},{3,7},{4,0},{5,1},{6,2},{7,3},{8,12},{9,13},{10,... | collective-permute-start | bytes 393224 | tf_op jit(solution)/shard_map/ppermute | solution.py:274
  20.3 17.6 %collective-permute-start.10 = (f32[64,512]{1,0:T(8,128)S(1)}, f32[64,512]{1,0:T(8,128)S(1)}, u32[]{:S(2)}, u32[]{:S(2)}) collective-permute-start(f32[64,512]{1,0:T(8,128)S(1)} %get-tuple-element.50.refs_13_), channel_id=1, source_target_pairs={{0,4},{1,5},{2,6},{3,7},{4,0},{5,1},{6,2},{7,3},{8,12},{9,13},{10,... | collective-permute-start | bytes 393224 | tf_op jit(solution)/shard_map/ppermute | solution.py:274
  20.6 17.4 %collective-permute-start.11 = (f32[64,512]{1,0:T(8,128)S(1)}, f32[64,512]{1,0:T(8,128)S(1)}, u32[]{:S(2)}, u32[]{:S(2)}) collective-permute-start(f32[64,512]{1,0:T(8,128)S(1)} %get-tuple-element.50.refs_13_), channel_id=1, source_target_pairs={{0,4},{1,5},{2,6},{3,7},{4,0},{5,1},{6,2},{7,3},{8,12},{9,13},{10,... | collective-permute-start | bytes 393224 | tf_op jit(solution)/shard_map/ppermute | solution.py:274
  35.1 6.1 %collective-permute-start.3 = (f32[128,512]{1,0:T(8,128)S(1)}, f32[128,512]{1,0:T(8,128)S(1)}, u32[]{:S(2)}, u32[]{:S(2)}) collective-permute-start(f32[128,512]{1,0:T(8,128)S(1)} %slice.6), channel_id=1, source_target_pairs={{0,4},{1,5},{2,6},{3,7},{4,0},{5,1},{6,2},{7,3},{8,12},{9,13},{10,... | collective-permute-start | bytes 786440 | tf_op jit(solution)/shard_map/ppermute | solution.py:274
  37.9 9.2 %collective-permute-start.4 = (f32[128,512]{1,0:T(8,128)S(1)}, f32[128,512]{1,0:T(8,128)S(1)}, u32[]{:S(2)}, u32[]{:S(2)}) collective-permute-start(f32[128,512]{1,0:T(8,128)S(1)} %slice.6), channel_id=1, source_target_pairs={{0,4},{1,5},{2,6},{3,7},{4,0},{5,1},{6,2},{7,3},{8,12},{9,13},{10,... | collective-permute-start | bytes 786440 | tf_op jit(solution)/shard_map/ppermute | solution.py:274
  37.9 9.2 %collective-permute-start.5 = (f32[128,512]{1,0:T(8,128)S(1)}, f32[128,512]{1,0:T(8,128)S(1)}, u32[]{:S(2)}, u32[]{:S(2)}) collective-permute-start(f32[128,512]{1,0:T(8,128)S(1)} %slice.6), channel_id=1, source_target_pairs={{0,4},{1,5},{2,6},{3,7},{4,0},{5,1},{6,2},{7,3},{8,12},{9,13},{10,... | collective-permute-start | bytes 786440 | tf_op jit(solution)/shard_map/ppermute | solution.py:274
  41.2 6.5 %collective-permute-start.12 = (f32[64,512]{1,0:T(8,128)S(1)}, f32[64,512]{1,0:T(8,128)S(1)}, u32[]{:S(2)}, u32[]{:S(2)}) collective-permute-start(f32[64,512]{1,0:T(8,128)S(1)} %shard_map.54.refs_12_), channel_id=1, source_target_pairs={{0,4},{1,5},{2,6},{3,7},{4,0},{5,1},{6,2},{7,3},{8,12},{9,13},{10,... | collective-permute-start | bytes 393224 | tf_op jit(solution)/shard_map/ppermute | solution.py:274
  47.9 1.4 %collective-permute-start.13 = (f32[64,512]{1,0:T(8,128)S(1)}, f32[64,512]{1,0:T(8,128)S(1)}, u32[]{:S(2)}, u32[]{:S(2)}) collective-permute-start(f32[64,512]{1,0:T(8,128)S(1)} %get-tuple-element.52), channel_id=1, source_target_pairs={{0,4},{1,5},{2,6},{3,7},{4,0},{5,1},{6,2},{7,3},{8,12},{9,13},{10,... | collective-permute-start | bytes 393224 | tf_op jit(solution)/shard_map/ppermute | solution.py:274
  49.4 6.5 %collective-permute-start.14 = (f32[64,512]{1,0:T(8,128)S(1)}, f32[64,512]{1,0:T(8,128)S(1)}, u32[]{:S(2)}, u32[]{:S(2)}) collective-permute-start(f32[64,512]{1,0:T(8,128)S(1)} %get-tuple-element.54), channel_id=1, source_target_pairs={{0,4},{1,5},{2,6},{3,7},{4,0},{5,1},{6,2},{7,3},{8,12},{9,13},{10,... | collective-permute-start | bytes 393224 | tf_op jit(solution)/shard_map/ppermute | solution.py:274
  56.3 1.4 %collective-permute-start.15 = (f32[64,512]{1,0:T(8,128)S(1)}, f32[64,512]{1,0:T(8,128)S(1)}, u32[]{:S(2)}, u32[]{:S(2)}) collective-permute-start(f32[64,512]{1,0:T(8,128)S(1)} %get-tuple-element.55), channel_id=1, source_target_pairs={{0,4},{4,0},{1,5},{5,1},{2,6},{6,2},{3,7},{7,3},{8,12},{12,8},{9,1... | collective-permute-start | bytes 393224 | tf_op jit(solution)/shard_map/ppermute | solution.py:315

commit v5 on v4

--- a/solution.py
+++ b/solution.py
@@ -180,36 +180,75 @@
             end_ref[...] = current
 
 
-def final_body(chips, me_ref, *refs):
-    maps, (walked_ref, walk_end_ref, had_ref) = refs[:12], refs[12:15]
-    news, (in_ref, end_ref) = refs[15:-2], refs[-2:]
+def ahead_body(me_ref, *refs):
+    maps, (hi_ref, lo_ref, vec_ref) = refs[:12], refs[12:]
+    for z, x, count in [(2, x, 4) for x in range(4)] + [(3, x, x) for x in range(1, 4)]:
+        @pl.when((me_ref[0] >> 2) == 8 * z + 2 * x + 1)
+        def _():
+            hi, lo, vec = (r[...] for r in maps[3 * (-x % 4):][:3])
+            for chip in range(1, count):
+                later = [r[...] for r in maps[3 * ((chip - x) % 4):][:3]]
+                vec = later[2] + mm(split(vec), later[:2])
+                hi, lo = split(mm((hi, lo), later[:2]))
+            hi_ref[...], lo_ref[...], vec_ref[...] = hi, lo, vec
+
+
+def cross_body(chips, me_ref, had_ref, *refs):
+    *news, hi_ref, lo_ref, vec_ref, in_ref, end_ref = refs
+    inflow = arrived(me_ref, had_ref[...], list(zip(news, chips)))
+    in_ref[...] = inflow
+
+    @pl.when(upper_only(me_ref) & ((me_ref[0] >> 5) == 2))
+    def _():
+        end_ref[...] = vec_ref[...] + mm(split(inflow), (hi_ref[...], lo_ref[...]))
+
+
+def inner_body(me_ref, *refs):
+    maps, had_ref, in_ref = refs[:12], refs[12], refs[13]
     line = me_ref[0] >> 5
-
-    @pl.when(line == 0)
-    def _():
-        in_ref[...] = walked_ref[...]
-        end_ref[...] = walk_end_ref[...]
-
     for x in range(4):
-        @pl.when(upper_only(me_ref) & (((me_ref[0] >> 3) & 3) == x))
+        @pl.when(upper_only(me_ref) & (line < 3) & (((me_ref[0] >> 3) & 3) == x))
         def _():
-            current = arrived(me_ref, had_ref[...], list(zip(news, chips)))
-            for chip in range(x + 1):
-                if chip == x:
-                    in_ref[...] = current
+            current = had_ref[...]
+            for chip in range(x):
                 hi, lo, vec = maps[3 * ((chip - x) % 4):][:3]
                 current = vec[...] + mm(split(current), (hi[...], lo[...]))
-            end_ref[...] = current
-
-
-def last_body(me_ref, in_ref, end_ref, own_ref, out_ref):
+            in_ref[...] = current
+
+
+def final_body(me_ref, ahead_hi_ref, ahead_lo_ref, ahead_vec_ref, walked_ref, inner_ref, got_ref, in_ref):
+    line = me_ref[0] >> 5
+    x = (me_ref[0] >> 3) & 3
+
+    @pl.when(line == 0)
+    def _():
+        in_ref[...] = walked_ref[...]
+
+    @pl.when((line == 1) | (line == 2))
+    def _():
+        in_ref[...] = inner_ref[...]
+
+    @pl.when((line == 3) & (x == 0))
+    def _():
+        in_ref[...] = got_ref[...]
+
+    @pl.when((line == 3) & (x > 0) & (core_of(me_ref) == 1))
+    def _():
+        in_ref[...] = ahead_vec_ref[...] + mm(split(got_ref[...]), (ahead_hi_ref[...], ahead_lo_ref[...]))
+
+
+def last_body(me_ref, down_ref, in_ref, own_ref, hi_ref, lo_ref, vec_ref, walk_end_ref, out_ref):
     @pl.when(core_of(me_ref) == 0)
     def _():
-        out_ref[...] = own_ref[N:, :] + mm(split(in_ref[...]), split(own_ref[:N, :]))
-
-    @pl.when(core_of(me_ref) == 1)
-    def _():
-        out_ref[...] = end_ref[...]
+        out_ref[...] = own_ref[N:, :] + mm(split(down_ref[...]), split(own_ref[:N, :]))
+
+    @pl.when((core_of(me_ref) == 1) & (me_ref[0] < 32))
+    def _():
+        out_ref[...] = walk_end_ref[...]
+
+    @pl.when(upper_only(me_ref))
+    def _():
+        out_ref[...] = vec_ref[...] + mm(split(in_ref[...]), (hi_ref[...], lo_ref[...]))
 
 
 def kernel(body, outs, scratch=(), space=pltpu.VMEM):
@@ -307,13 +346,15 @@
     line = kernel(functools.partial(line_body, 1, [(5, 6)]), two)
     inflow, end = line(me, *maps, inflow, third)
     fourth = send(end, hops([((1, x), (2, x)) for x in range(4)]))
-    line = kernel(functools.partial(line_body, 2, [(8, 9, 10, 11)]), two)
-    inflow, end = line(me, *maps, inflow, fourth)
+    ahead = kernel(ahead_body, weights)(me, *maps)
+    cross = kernel(functools.partial(cross_body, [(8, 9, 10, 11)]), two)
+    inflow, end = cross(me, inflow, fourth, *ahead)
     fifth = send(end, hops([((2, x), (3, x)) for x in range(4)]))
-    inflow, end = kernel(functools.partial(final_body, [(12, 13, 14, 15)]), two)(
-        me, *maps, walked, walk_end, inflow, fifth)
+    inner = kernel(inner_body, arr(R))(me, *maps, inflow)
+    inflow = kernel(final_body, arr(R))(me, *ahead, walked, inner, fifth)
     down = lax.ppermute(inflow, "c", [(0, 1), (1, 0)])
-    return kernel(last_body, jax.ShapeDtypeStruct((R, N), F32))(me, down, end, own)
+    return kernel(last_body, jax.ShapeDtypeStruct((R, N), F32))(
+        me, down, inflow, own, hi, lo, vec, walk_end)
 
 
 def solution(mesh):

time: 58.6 us -> 55.5 us (0.947)
  the two profiles are of different devices: /device:TPU:97 before, /device:TPU:115 now
where the time goes in v5:
time: 55.5 us; the launch traced here: 55.4 us
  waiting for transfers between devices  35 us (63%)
  starting transfers between devices  11.7 us (21%)
  Pallas kernels  8.53 us (15%)
    ppermute x14, waiting for transfers between devices, send(): return lax.ppermute(value, ALL, pairs)  31.2 us
    ppermute x14, starting transfers between devices, send(): return lax.ppermute(value, ALL, pairs)  10.8 us
    pallas_call x15, Pallas kernels, call(): pl.pallas_call(body, out_shape=outs, in_specs=[smem if a.dtype == jnp.int...  8.53 us
    ppermute x1, waiting for transfers between devices, local(): other = lax.ppermute(own, 'c', [(0, 1), (1, 0)])  2.47 us
    ppermute x1, waiting for transfers between devices, local(): down = lax.ppermute(inflow, 'c', [(0, 1), (1, 0)])  1.33 us
  transfers between devices with their start and end apart: 16, of which 9 were waited for; matrix products, arithmetic and copies ran while one was open for 0% of the time, Pallas kernels for 1%

profile of v5, /device:TPU:115, one launch (start us, length us, event | category | flops | bytes accessed | tf_op | source)
XLA Modules:
  0.0 55.4 jit_solution(5154414114666569868)
XLA Ops:
  0.0 4.8 %shard_map.46.own_ref = f32[576,512]{1,0:T(8,128)S(1)} custom-call(s32[1]{0:T(128)} %bitcast.me_ref, f32[1,512,512]{2,1,0:T(8,128)} %diag_hbm.1, f32[1,512,512]{2,1,0:T(8,128)} %sub_hbm.1, f32[64,512]{1,0:T(8,128)} %right_hbm.1, f32[64,512]{1,0:T(8,128)} %bitcast.2), custom_call_target="tpu_custom_call" | custom-call | tf_op jit(solution)/shard_map/pallas_call | solution.py:260
  4.8 0.8 %collective-permute-start = (f32[576,512]{1,0:T(8,128)S(1)}, f32[576,512]{1,0:T(8,128)S(1)}, u32[]{:S(2)}, u32[]{:S(2)}) collective-permute-start(f32[576,512]{1,0:T(8,128)S(1)} %shard_map.46.own_ref), channel_id=1, source_target_pairs={{0,4},{4,0},{1,5},{5,1},{2,6},{6,2},{3,7},{7,3},{8,12},{12,8},{9,1... | collective-permute-start | bytes 3538952 | tf_op jit(solution)/shard_map/ppermute | solution.py:322
  5.5 2.5 %collective-permute-done.other_ref = f32[576,512]{1,0:T(8,128)S(1)} collective-permute-done((f32[576,512]{1,0:T(8,128)S(1)}, f32[576,512]{1,0:T(8,128)S(1)}, u32[]{:S(2)}, u32[]{:S(2)}) %collective-permute-start) | collective-permute-done | bytes 1179680 | tf_op jit(solution)/shard_map/ppermute | solution.py:322
  8.0 1.1 %shard_map.47 = (f32[576,512]{1,0:T(8,128)S(1)}, f32[192,512]{1,0:T(8,128)S(1)}, bf16[512,512]{1,0:T(8,128)(2,1)S(1)}, bf16[512,512]{1,0:T(8,128)(2,1)S(1)}, f32[64,512]{1,0:T(8,128)S(1)}) custom-call(s32[1]{0:T(128)} %bitcast.me_ref, f32[576,512]{1,0:T(8,128)S(1)} %shard_map.46.own_ref, f32[576,512]{1,0:T(8,128)S(1)} %collective-permute-done.other_ref), custom_call_target="tpu_custom_call" | custom-call | tf_op jit(solution)/shard_map/pallas_call | solution.py:260
  9.2 3.1 %collective-permute-start.6 = (f32[576,512]{1,0:T(8,128)S(1)}, f32[576,512]{1,0:T(8,128)S(1)}, u32[]{:S(2)}, u32[]{:S(2)}) collective-permute-start(f32[576,512]{1,0:T(8,128)S(1)} %get-tuple-element.35), channel_id=1, source_target_pairs={{60,36},{61,37},{62,38},{63,39},{36,44},{37,45},{38,46},{39,47},{4... | collective-permute-start | bytes 3538952 | tf_op jit(solution)/shard_map/ppermute | solution.py:313
  12.3 2.2 %collective-permute-start.1 = (f32[576,512]{1,0:T(8,128)S(1)}, f32[576,512]{1,0:T(8,128)S(1)}, u32[]{:S(2)}, u32[]{:S(2)}) collective-permute-start(f32[576,512]{1,0:T(8,128)S(1)} %get-tuple-element.35), channel_id=1, source_target_pairs={{44,36},{45,37},{46,38},{47,39},{52,44},{53,45},{54,46},{55,47},{6... | collective-permute-start | bytes 3538952 | tf_op jit(solution)/shard_map/ppermute | solution.py:313
  14.5 0.1 collective-permute-start.7
  14.5 1.9 %collective-permute-start.2 = (f32[192,512]{1,0:T(8,128)S(1)}, f32[192,512]{1,0:T(8,128)S(1)}, u32[]{:S(2)}, u32[]{:S(2)}) collective-permute-start(f32[192,512]{1,0:T(8,128)S(1)} %get-tuple-element.39), channel_id=1, source_target_pairs={{0,4},{1,5},{2,6},{3,7},{4,0},{5,1},{6,2},{7,3},{8,12},{9,13},{10,... | collective-permute-start | bytes 1179656 | tf_op jit(solution)/shard_map/ppermute | solution.py:313
  16.6 1.3 %collective-permute-done.8.got_ref = f32[64,512]{1,0:T(8,128)S(1)} collective-permute-done((f32[64,512]{1,0:T(8,128)S(1)}, f32[64,512]{1,0:T(8,128)S(1)}, u32[]{:S(2)}, u32[]{:S(2)}) %collective-permute-start.8) | collective-permute-done | bytes 131104 | tf_op jit(solution)/shard_map/ppermute | solution.py:313
  18.0 0.2 collective-permute-start.9
  18.2 1.2 %collective-permute-done.9.got_ref = f32[64,512]{1,0:T(8,128)S(1)} collective-permute-done((f32[64,512]{1,0:T(8,128)S(1)}, f32[64,512]{1,0:T(8,128)S(1)}, u32[]{:S(2)}, u32[]{:S(2)}) %collective-permute-start.9) | collective-permute-done | bytes 131104 | tf_op jit(solution)/shard_map/ppermute | solution.py:313
  19.4 0.2 collective-permute-start.11
  19.6 0.4 collective-permute-start.10
  20.0 14.1 %collective-permute-done.2.refs_0_ = f32[192,512]{1,0:T(8,128)S(1)} collective-permute-done((f32[192,512]{1,0:T(8,128)S(1)}, f32[192,512]{1,0:T(8,128)S(1)}, u32[]{:S(2)}, u32[]{:S(2)}) %collective-permute-start.2) | collective-permute-done | bytes 393248 | tf_op jit(solution)/shard_map/ppermute | solution.py:313
  34.1 0.1 collective-permute-start.5
  34.2 1.9 %collective-permute-start.4 = (f32[128,512]{1,0:T(8,128)S(1)}, f32[128,512]{1,0:T(8,128)S(1)}, u32[]{:S(2)}, u32[]{:S(2)}) collective-permute-start(f32[128,512]{1,0:T(8,128)S(1)} %slice.6), channel_id=1, source_target_pairs={{0,4},{1,5},{2,6},{3,7},{4,0},{5,1},{6,2},{7,3},{8,12},{9,13},{10,... | collective-permute-start | bytes 786440 | tf_op jit(solution)/shard_map/ppermute | solution.py:313
  36.1 0.3 collective-permute-start.3
  36.5 4.5 %collective-permute-done.5.refs_3_ = f32[128,512]{1,0:T(8,128)S(1)} collective-permute-done((f32[128,512]{1,0:T(8,128)S(1)}, f32[128,512]{1,0:T(8,128)S(1)}, u32[]{:S(2)}, u32[]{:S(2)}) %collective-permute-start.5) | collective-permute-done | bytes 262176 | tf_op jit(solution)/shard_map/ppermute | solution.py:313
  41.0 1.9 %collective-permute-done.4.refs_2_ = f32[128,512]{1,0:T(8,128)S(1)} collective-permute-done((f32[128,512]{1,0:T(8,128)S(1)}, f32[128,512]{1,0:T(8,128)S(1)}, u32[]{:S(2)}, u32[]{:S(2)}) %collective-permute-start.4) | collective-permute-done | bytes 262176 | tf_op jit(solution)/shard_map/ppermute | solution.py:313
  42.9 0.2 shard_map.49
  43.1 0.2 shard_map.50
  43.3 0.2 shard_map.48
  43.5 0.2 shard_map.56
  43.7 0.1 collective-permute-start.13
  43.8 0.1 shard_map.51
  44.0 1.2 %collective-permute-done.13.refs_0_ = f32[64,512]{1,0:T(8,128)S(1)} collective-permute-done((f32[64,512]{1,0:T(8,128)S(1)}, f32[64,512]{1,0:T(8,128)S(1)}, u32[]{:S(2)}, u32[]{:S(2)}) %collective-permute-start.13) | collective-permute-done | bytes 131104 | tf_op jit(solution)/shard_map/ppermute | solution.py:313
  45.2 0.2 shard_map.57
  45.4 0.2 collective-permute-start.14
  45.6 6.9 %collective-permute-done.14.got_ref = f32[64,512]{1,0:T(8,128)S(1)} collective-permute-done((f32[64,512]{1,0:T(8,128)S(1)}, f32[64,512]{1,0:T(8,128)S(1)}, u32[]{:S(2)}, u32[]{:S(2)}) %collective-permute-start.14) | collective-permute-done | bytes 131104 | tf_op jit(solution)/shard_map/ppermute | solution.py:313
  52.5 0.4 shard_map.59.in_ref
  53.0 1.3 %collective-permute-done.15.down_ref = f32[64,512]{1,0:T(8,128)S(1)} collective-permute-done((f32[64,512]{1,0:T(8,128)S(1)}, f32[64,512]{1,0:T(8,128)S(1)}, u32[]{:S(2)}, u32[]{:S(2)}) %collective-permute-start.15) | collective-permute-done | bytes 131104 | tf_op jit(solution)/shard_map/ppermute | solution.py:355
  54.3 1.0 %shard_map.60 = f32[64,512]{1,0:T(8,128)} custom-call(s32[1]{0:T(128)} %bitcast.me_ref, f32[64,512]{1,0:T(8,128)S(1)} %collective-permute-done.15.down_ref, f32[64,512]{1,0:T(8,128)S(1)} %shard_map.59.in_ref, f32[576,512]{1,0:T(8,128)S(1)} %shard_map.46.own_ref, bf16[512,512]{1,0:T(8,128)(2,1)S(1)} %get-tuple-element.32.refs_0_.hi_ref, ...), custom_call_target="tpu_custom_call" | custom-call | tf_op jit(solution)/shard_map/pallas_call | solution.py:260
  (17 shorter events, 0.3 us)
Async XLA Ops:
  4.8 3.2 %collective-permute-start = (f32[576,512]{1,0:T(8,128)S(1)}, f32[576,512]{1,0:T(8,128)S(1)}, u32[]{:S(2)}, u32[]{:S(2)}) collective-permute-start(f32[576,512]{1,0:T(8,128)S(1)} %shard_map.46.own_ref), channel_id=1, source_target_pairs={{0,4},{4,0},{1,5},{5,1},{2,6},{6,2},{3,7},{7,3},{8,12},{12,8},{9,1... | collective-permute-start | bytes 3538952 | tf_op jit(solution)/shard_map/ppermute | solution.py:322
  9.2 34.0 %collective-permute-start.6 = (f32[576,512]{1,0:T(8,128)S(1)}, f32[576,512]{1,0:T(8,128)S(1)}, u32[]{:S(2)}, u32[]{:S(2)}) collective-permute-start(f32[576,512]{1,0:T(8,128)S(1)} %get-tuple-element.35), channel_id=1, source_target_pairs={{60,36},{61,37},{62,38},{63,39},{36,44},{37,45},{38,46},{39,47},{4... | collective-permute-start | bytes 3538952 | tf_op jit(solution)/shard_map/ppermute | solution.py:313
  12.3 31.0 %collective-permute-start.1 = (f32[576,512]{1,0:T(8,128)S(1)}, f32[576,512]{1,0:T(8,128)S(1)}, u32[]{:S(2)}, u32[]{:S(2)}) collective-permute-start(f32[576,512]{1,0:T(8,128)S(1)} %get-tuple-element.35), channel_id=1, source_target_pairs={{44,36},{45,37},{46,38},{47,39},{52,44},{53,45},{54,46},{55,47},{6... | collective-permute-start | bytes 3538952 | tf_op jit(solution)/shard_map/ppermute | solution.py:313
  14.5 2.0 %collective-permute-start.7 = (f32[64,512]{1,0:T(8,128)S(1)}, f32[64,512]{1,0:T(8,128)S(1)}, u32[]{:S(2)}, u32[]{:S(2)}) collective-permute-start(f32[64,512]{1,0:T(8,128)S(1)} %get-tuple-element.34.refs_2_.old_ref.vec_ref), channel_id=1, source_target_pairs={{0,4},{1,5},{2,6},{3,7},{4,12},{5,13},{6,14},{7,15},{8,0},{9,1},{1... | collective-permute-start | bytes 393224 | tf_op jit(solution)/shard_map/ppermute | solution.py:313
  14.5 19.5 %collective-permute-start.2 = (f32[192,512]{1,0:T(8,128)S(1)}, f32[192,512]{1,0:T(8,128)S(1)}, u32[]{:S(2)}, u32[]{:S(2)}) collective-permute-start(f32[192,512]{1,0:T(8,128)S(1)} %get-tuple-element.39), channel_id=1, source_target_pairs={{0,4},{1,5},{2,6},{3,7},{4,0},{5,1},{6,2},{7,3},{8,12},{9,13},{10,... | collective-permute-start | bytes 1179656 | tf_op jit(solution)/shard_map/ppermute | solution.py:313
  16.5 1.4 %collective-permute-start.8 = (f32[64,512]{1,0:T(8,128)S(1)}, f32[64,512]{1,0:T(8,128)S(1)}, u32[]{:S(2)}, u32[]{:S(2)}) collective-permute-start(f32[64,512]{1,0:T(8,128)S(1)} %get-tuple-element.49.old_ref), channel_id=1, source_target_pairs={{0,4},{1,5},{2,6},{3,7},{4,0},{5,1},{6,2},{7,3},{8,12},{9,13},{10,... | collective-permute-start | bytes 393224 | tf_op jit(solution)/shard_map/ppermute | solution.py:313
  18.0 1.4 %collective-permute-start.9 = (f32[64,512]{1,0:T(8,128)S(1)}, f32[64,512]{1,0:T(8,128)S(1)}, u32[]{:S(2)}, u32[]{:S(2)}) collective-permute-start(f32[64,512]{1,0:T(8,128)S(1)} %get-tuple-element.51.old_ref), channel_id=1, source_target_pairs={{0,4},{1,5},{2,6},{3,7},{4,0},{5,1},{6,2},{7,3},{8,12},{9,13},{10,... | collective-permute-start | bytes 393224 | tf_op jit(solution)/shard_map/ppermute | solution.py:313
  19.4 14.8 %collective-permute-start.11 = (f32[64,512]{1,0:T(8,128)S(1)}, f32[64,512]{1,0:T(8,128)S(1)}, u32[]{:S(2)}, u32[]{:S(2)}) collective-permute-start(f32[64,512]{1,0:T(8,128)S(1)} %get-tuple-element.54.walk_end_ref), channel_id=1, source_target_pairs={{0,4},{1,5},{2,6},{3,7},{4,0},{5,1},{6,2},{7,3},{8,12},{9,13},{10,... | collective-permute-start | bytes 393224 | tf_op jit(solution)/shard_map/ppermute | solution.py:313
  19.6 16.5 %collective-permute-start.10 = (f32[64,512]{1,0:T(8,128)S(1)}, f32[64,512]{1,0:T(8,128)S(1)}, u32[]{:S(2)}, u32[]{:S(2)}) collective-permute-start(f32[64,512]{1,0:T(8,128)S(1)} %get-tuple-element.54.walk_end_ref), channel_id=1, source_target_pairs={{0,4},{1,5},{2,6},{3,7},{4,0},{5,1},{6,2},{7,3},{8,12},{9,13},{10,... | collective-permute-start | bytes 393224 | tf_op jit(solution)/shard_map/ppermute | solution.py:313
  34.1 6.9 %collective-permute-start.5 = (f32[128,512]{1,0:T(8,128)S(1)}, f32[128,512]{1,0:T(8,128)S(1)}, u32[]{:S(2)}, u32[]{:S(2)}) collective-permute-start(f32[128,512]{1,0:T(8,128)S(1)} %slice.6), channel_id=1, source_target_pairs={{0,4},{1,5},{2,6},{3,7},{4,0},{5,1},{6,2},{7,3},{8,12},{9,13},{10,... | collective-permute-start | bytes 786440 | tf_op jit(solution)/shard_map/ppermute | solution.py:313
  34.2 8.7 %collective-permute-start.4 = (f32[128,512]{1,0:T(8,128)S(1)}, f32[128,512]{1,0:T(8,128)S(1)}, u32[]{:S(2)}, u32[]{:S(2)}) collective-permute-start(f32[128,512]{1,0:T(8,128)S(1)} %slice.6), channel_id=1, source_target_pairs={{0,4},{1,5},{2,6},{3,7},{4,0},{5,1},{6,2},{7,3},{8,12},{9,13},{10,... | collective-permute-start | bytes 786440 | tf_op jit(solution)/shard_map/ppermute | solution.py:313
  36.1 6.8 %collective-permute-start.3 = (f32[128,512]{1,0:T(8,128)S(1)}, f32[128,512]{1,0:T(8,128)S(1)}, u32[]{:S(2)}, u32[]{:S(2)}) collective-permute-start(f32[128,512]{1,0:T(8,128)S(1)} %slice.6), channel_id=1, source_target_pairs={{0,4},{1,5},{2,6},{3,7},{4,0},{5,1},{6,2},{7,3},{8,12},{9,13},{10,... | collective-permute-start | bytes 786440 | tf_op jit(solution)/shard_map/ppermute | solution.py:313
  41.0 2.5 %collective-permute-start.12 = (f32[64,512]{1,0:T(8,128)S(1)}, f32[64,512]{1,0:T(8,128)S(1)}, u32[]{:S(2)}, u32[]{:S(2)}) collective-permute-start(f32[64,512]{1,0:T(8,128)S(1)} %shard_map.55.refs_12_), channel_id=1, source_target_pairs={{0,4},{1,5},{2,6},{3,7},{4,0},{5,1},{6,2},{7,3},{8,12},{9,13},{10,... | collective-permute-start | bytes 393224 | tf_op jit(solution)/shard_map/ppermute | solution.py:313
  43.7 1.4 %collective-permute-start.13 = (f32[64,512]{1,0:T(8,128)S(1)}, f32[64,512]{1,0:T(8,128)S(1)}, u32[]{:S(2)}, u32[]{:S(2)}) collective-permute-start(f32[64,512]{1,0:T(8,128)S(1)} %get-tuple-element.56), channel_id=1, source_target_pairs={{0,4},{1,5},{2,6},{3,7},{4,0},{5,1},{6,2},{7,3},{8,12},{9,13},{10,... | collective-permute-start | bytes 393224 | tf_op jit(solution)/shard_map/ppermute | solution.py:313
  45.4 7.1 %collective-permute-start.14 = (f32[64,512]{1,0:T(8,128)S(1)}, f32[64,512]{1,0:T(8,128)S(1)}, u32[]{:S(2)}, u32[]{:S(2)}) collective-permute-start(f32[64,512]{1,0:T(8,128)S(1)} %get-tuple-element.58), channel_id=1, source_target_pairs={{0,4},{1,5},{2,6},{3,7},{4,0},{5,1},{6,2},{7,3},{8,12},{9,13},{10,... | collective-permute-start | bytes 393224 | tf_op jit(solution)/shard_map/ppermute | solution.py:313
  52.9 1.4 %collective-permute-start.15 = (f32[64,512]{1,0:T(8,128)S(1)}, f32[64,512]{1,0:T(8,128)S(1)}, u32[]{:S(2)}, u32[]{:S(2)}) collective-permute-start(f32[64,512]{1,0:T(8,128)S(1)} %shard_map.59.in_ref), channel_id=1, source_target_pairs={{0,4},{4,0},{1,5},{5,1},{2,6},{6,2},{3,7},{7,3},{8,12},{12,8},{9,1... | collective-permute-start | bytes 393224 | tf_op jit(solution)/shard_map/ppermute | solution.py:355

commit v6 on v5

--- a/solution.py
+++ b/solution.py
@@ -40,15 +40,18 @@
     return both[:, :Q] + both[:, Q:]
 
 
-def local_body(me_ref, diag_hbm, sub_hbm, right_hbm, bound_hbm, out_ref, diag_ref, sub_ref, right_ref, bound_ref, sems):
+def local_body(me_ref, diag_hbm, sub_hbm, right_hbm, bound_hbm, out_ref, diag_ref, sub_ref, right_ref, bound_ref, ups_ref, sems):
     loads = [
         pltpu.make_async_copy(src, dst, sems.at[i])
         for i, (src, dst) in enumerate([
             (diag_hbm, diag_ref), (sub_hbm, sub_ref), (right_hbm, right_ref), (bound_hbm, bound_ref)])
     ]
-    for load in loads:
+    spans = [slice(i * Q, (i + 1) * Q) for i in range(4)]
+    blocks = [pltpu.make_async_copy(diag_hbm.at[0, r, r], ups_ref.at[i], sems.at[4 + i]) for i, r in enumerate(spans)]
+    for load in blocks + loads:
         load.start()
-    loads[0].wait()
+    for load in blocks:
+        load.wait()
     row = lax.broadcasted_iota(jnp.int32, (Q, Q), 0)
     col = lax.broadcasted_iota(jnp.int32, (Q, Q), 1)
     eye = row == col
@@ -56,7 +59,7 @@
     def block(i, j):
         return diag_ref[0, j * Q:(j + 1) * Q, i * Q:(i + 1) * Q].T
 
-    ups = [block(i, i) for i in range(4)]
+    ups = [ups_ref[i].T for i in range(4)]
     inv = []
     for u in ups:
         d = jnp.where(eye, u, 0.0)
@@ -69,6 +72,7 @@
         pick = ((rb & 1) == 0) & (cb == rb + 1)
         half = [mm_small(x, jnp.where(pick, u, 0.0)) for x, u in zip(inv, ups)]
         inv = [x - mm_small(h, x) for h, x in zip(half, inv)]
+    loads[0].wait()
     tiles = []
     for i in (0, 2):
         off = mm_small(mm_small(inv[i], block(i, i + 1)), inv[i + 1])
@@ -106,10 +110,6 @@
         full_ref[N:, :] = vec
         vec_ref[...] = vec
 
-    @pl.when(core_of(me_ref) == 0)
-    def _():
-        go(own_ref, other_ref)
-
     @pl.when(core_of(me_ref) == 1)
     def _():
         go(other_ref, own_ref)
@@ -315,7 +315,7 @@
     me = lax.axis_index(ALL).astype(jnp.int32).reshape(1)
     loads = [
         pltpu.VMEM((1, N, N), F32), pltpu.VMEM((1, N, N), F32), pltpu.VMEM((R, N), F32),
-        pltpu.VMEM((R, N), F32), pltpu.SemaphoreType.DMA((4,)),
+        pltpu.VMEM((R, N), F32), pltpu.VMEM((4, Q, Q), F32), pltpu.SemaphoreType.DMA((8,)),
     ]
     own = kernel(local_body, arr(N + R), loads, pltpu.HBM)(
         me, diag_blocks, sub_blocks, right_side, boundary.T)

time: 55.5 us -> 55.1 us (level)
  no operation moved by 1% of the time
where the time goes in v6:
time: 55.1 us; the launch traced here: 55 us
  waiting for transfers between devices  35 us (64%)
  starting transfers between devices  11.7 us (21%)
  Pallas kernels  8.09 us (15%)
    ppermute x14, waiting for transfers between devices, send(): return lax.ppermute(value, ALL, pairs)  31.2 us
    ppermute x14, starting transfers between devices, send(): return lax.ppermute(value, ALL, pairs)  10.8 us
    pallas_call x15, Pallas kernels, call(): pl.pallas_call(body, out_shape=outs, in_specs=[smem if a.dtype == jnp.int...  8.09 us
    ppermute x1, waiting for transfers between devices, local(): other = lax.ppermute(own, 'c', [(0, 1), (1, 0)])  2.47 us
    ppermute x1, waiting for transfers between devices, local(): down = lax.ppermute(inflow, 'c', [(0, 1), (1, 0)])  1.33 us
  transfers between devices with their start and end apart: 16, of which 9 were waited for; matrix products, arithmetic and copies ran while one was open for 0% of the time, Pallas kernels for 1%

profile of v6, /device:TPU:115, one launch (start us, length us, event | category | flops | bytes accessed | tf_op | source)
XLA Modules:
  0.0 55.0 jit_solution(7146080288870398357)
XLA Ops:
  0.0 4.5 %shard_map.46.own_ref = f32[576,512]{1,0:T(8,128)S(1)} custom-call(s32[1]{0:T(128)} %bitcast.me_ref, f32[1,512,512]{2,1,0:T(8,128)} %diag_hbm.1, f32[1,512,512]{2,1,0:T(8,128)} %sub_hbm.1, f32[64,512]{1,0:T(8,128)} %right_hbm.1, f32[64,512]{1,0:T(8,128)} %bitcast.2), custom_call_target="tpu_custom_call" | custom-call | tf_op jit(solution)/shard_map/pallas_call | solution.py:260
  4.6 0.8 %collective-permute-start = (f32[576,512]{1,0:T(8,128)S(1)}, f32[576,512]{1,0:T(8,128)S(1)}, u32[]{:S(2)}, u32[]{:S(2)}) collective-permute-start(f32[576,512]{1,0:T(8,128)S(1)} %shard_map.46.own_ref), channel_id=1, source_target_pairs={{0,4},{4,0},{1,5},{5,1},{2,6},{6,2},{3,7},{7,3},{8,12},{12,8},{9,1... | collective-permute-start | bytes 3538952 | tf_op jit(solution)/shard_map/ppermute | solution.py:322
  5.3 2.5 %collective-permute-done.other_ref = f32[576,512]{1,0:T(8,128)S(1)} collective-permute-done((f32[576,512]{1,0:T(8,128)S(1)}, f32[576,512]{1,0:T(8,128)S(1)}, u32[]{:S(2)}, u32[]{:S(2)}) %collective-permute-start) | collective-permute-done | bytes 1179680 | tf_op jit(solution)/shard_map/ppermute | solution.py:322
  7.8 1.1 %shard_map.47 = (f32[576,512]{1,0:T(8,128)S(1)}, f32[192,512]{1,0:T(8,128)S(1)}, bf16[512,512]{1,0:T(8,128)(2,1)S(1)}, bf16[512,512]{1,0:T(8,128)(2,1)S(1)}, f32[64,512]{1,0:T(8,128)S(1)}) custom-call(s32[1]{0:T(128)} %bitcast.me_ref, f32[576,512]{1,0:T(8,128)S(1)} %shard_map.46.own_ref, f32[576,512]{1,0:T(8,128)S(1)} %collective-permute-done.other_ref), custom_call_target="tpu_custom_call" | custom-call | tf_op jit(solution)/shard_map/pallas_call | solution.py:260
  8.9 3.1 %collective-permute-start.6 = (f32[576,512]{1,0:T(8,128)S(1)}, f32[576,512]{1,0:T(8,128)S(1)}, u32[]{:S(2)}, u32[]{:S(2)}) collective-permute-start(f32[576,512]{1,0:T(8,128)S(1)} %get-tuple-element.35), channel_id=1, source_target_pairs={{60,36},{61,37},{62,38},{63,39},{36,44},{37,45},{38,46},{39,47},{4... | collective-permute-start | bytes 3538952 | tf_op jit(solution)/shard_map/ppermute | solution.py:313
  12.1 2.2 %collective-permute-start.1 = (f32[576,512]{1,0:T(8,128)S(1)}, f32[576,512]{1,0:T(8,128)S(1)}, u32[]{:S(2)}, u32[]{:S(2)}) collective-permute-start(f32[576,512]{1,0:T(8,128)S(1)} %get-tuple-element.35), channel_id=1, source_target_pairs={{44,36},{45,37},{46,38},{47,39},{52,44},{53,45},{54,46},{55,47},{6... | collective-permute-start | bytes 3538952 | tf_op jit(solution)/shard_map/ppermute | solution.py:313
  14.2 0.1 collective-permute-start.7
  14.3 1.9 %collective-permute-start.2 = (f32[192,512]{1,0:T(8,128)S(1)}, f32[192,512]{1,0:T(8,128)S(1)}, u32[]{:S(2)}, u32[]{:S(2)}) collective-permute-start(f32[192,512]{1,0:T(8,128)S(1)} %get-tuple-element.39), channel_id=1, source_target_pairs={{0,4},{1,5},{2,6},{3,7},{4,0},{5,1},{6,2},{7,3},{8,12},{9,13},{10,... | collective-permute-start | bytes 1179656 | tf_op jit(solution)/shard_map/ppermute | solution.py:313
  16.3 0.1 collective-permute-start.8
  16.4 1.3 %collective-permute-done.8.got_ref = f32[64,512]{1,0:T(8,128)S(1)} collective-permute-done((f32[64,512]{1,0:T(8,128)S(1)}, f32[64,512]{1,0:T(8,128)S(1)}, u32[]{:S(2)}, u32[]{:S(2)}) %collective-permute-start.8) | collective-permute-done | bytes 131104 | tf_op jit(solution)/shard_map/ppermute | solution.py:313
  17.7 0.2 collective-permute-start.9
  18.0 1.2 %collective-permute-done.9.got_ref = f32[64,512]{1,0:T(8,128)S(1)} collective-permute-done((f32[64,512]{1,0:T(8,128)S(1)}, f32[64,512]{1,0:T(8,128)S(1)}, u32[]{:S(2)}, u32[]{:S(2)}) %collective-permute-start.9) | collective-permute-done | bytes 131104 | tf_op jit(solution)/shard_map/ppermute | solution.py:313
  19.2 0.2 collective-permute-start.11
  19.4 0.4 collective-permute-start.10
  19.8 14.1 %collective-permute-done.2.refs_0_ = f32[192,512]{1,0:T(8,128)S(1)} collective-permute-done((f32[192,512]{1,0:T(8,128)S(1)}, f32[192,512]{1,0:T(8,128)S(1)}, u32[]{:S(2)}, u32[]{:S(2)}) %collective-permute-start.2) | collective-permute-done | bytes 393248 | tf_op jit(solution)/shard_map/ppermute | solution.py:313
  33.9 0.1 collective-permute-start.5
  34.0 1.9 %collective-permute-start.4 = (f32[128,512]{1,0:T(8,128)S(1)}, f32[128,512]{1,0:T(8,128)S(1)}, u32[]{:S(2)}, u32[]{:S(2)}) collective-permute-start(f32[128,512]{1,0:T(8,128)S(1)} %slice.6), channel_id=1, source_target_pairs={{0,4},{1,5},{2,6},{3,7},{4,0},{5,1},{6,2},{7,3},{8,12},{9,13},{10,... | collective-permute-start | bytes 786440 | tf_op jit(solution)/shard_map/ppermute | solution.py:313
  35.9 0.3 collective-permute-start.3
  36.2 4.5 %collective-permute-done.5.refs_3_ = f32[128,512]{1,0:T(8,128)S(1)} collective-permute-done((f32[128,512]{1,0:T(8,128)S(1)}, f32[128,512]{1,0:T(8,128)S(1)}, u32[]{:S(2)}, u32[]{:S(2)}) %collective-permute-start.5) | collective-permute-done | bytes 262176 | tf_op jit(solution)/shard_map/ppermute | solution.py:313
  40.8 1.9 %collective-permute-done.4.refs_2_ = f32[128,512]{1,0:T(8,128)S(1)} collective-permute-done((f32[128,512]{1,0:T(8,128)S(1)}, f32[128,512]{1,0:T(8,128)S(1)}, u32[]{:S(2)}, u32[]{:S(2)}) %collective-permute-start.4) | collective-permute-done | bytes 262176 | tf_op jit(solution)/shard_map/ppermute | solution.py:313
  42.7 0.2 shard_map.49
  42.9 0.2 shard_map.50
  43.1 0.2 shard_map.48
  43.3 0.2 shard_map.56
  43.5 0.1 collective-permute-start.13
  43.6 0.1 shard_map.51
  43.7 1.2 %collective-permute-done.13.refs_0_ = f32[64,512]{1,0:T(8,128)S(1)} collective-permute-done((f32[64,512]{1,0:T(8,128)S(1)}, f32[64,512]{1,0:T(8,128)S(1)}, u32[]{:S(2)}, u32[]{:S(2)}) %collective-permute-start.13) | collective-permute-done | bytes 131104 | tf_op jit(solution)/shard_map/ppermute | solution.py:313
  45.0 0.2 collective-permute-start.14
  45.2 6.9 %collective-permute-done.14.got_ref = f32[64,512]{1,0:T(8,128)S(1)} collective-permute-done((f32[64,512]{1,0:T(8,128)S(1)}, f32[64,512]{1,0:T(8,128)S(1)}, u32[]{:S(2)}, u32[]{:S(2)}) %collective-permute-start.14) | collective-permute-done | bytes 131104 | tf_op jit(solution)/shard_map/ppermute | solution.py:313
  52.1 0.4 shard_map.59.in_ref
  52.6 1.3 %collective-permute-done.15.down_ref = f32[64,512]{1,0:T(8,128)S(1)} collective-permute-done((f32[64,512]{1,0:T(8,128)S(1)}, f32[64,512]{1,0:T(8,128)S(1)}, u32[]{:S(2)}, u32[]{:S(2)}) %collective-permute-start.15) | collective-permute-done | bytes 131104 | tf_op jit(solution)/shard_map/ppermute | solution.py:355
  53.9 1.0 %shard_map.60 = f32[64,512]{1,0:T(8,128)} custom-call(s32[1]{0:T(128)} %bitcast.me_ref, f32[64,512]{1,0:T(8,128)S(1)} %collective-permute-done.15.down_ref, f32[64,512]{1,0:T(8,128)S(1)} %shard_map.59.in_ref, f32[576,512]{1,0:T(8,128)S(1)} %shard_map.46.own_ref, bf16[512,512]{1,0:T(8,128)(2,1)S(1)} %get-tuple-element.32.refs_0_.hi_ref, ...), custom_call_target="tpu_custom_call" | custom-call | tf_op jit(solution)/shard_map/pallas_call | solution.py:260
  (17 shorter events, 0.2 us)
Async XLA Ops:
  4.6 3.2 %collective-permute-start = (f32[576,512]{1,0:T(8,128)S(1)}, f32[576,512]{1,0:T(8,128)S(1)}, u32[]{:S(2)}, u32[]{:S(2)}) collective-permute-start(f32[576,512]{1,0:T(8,128)S(1)} %shard_map.46.own_ref), channel_id=1, source_target_pairs={{0,4},{4,0},{1,5},{5,1},{2,6},{6,2},{3,7},{7,3},{8,12},{12,8},{9,1... | collective-permute-start | bytes 3538952 | tf_op jit(solution)/shard_map/ppermute | solution.py:322
  8.9 34.0 %collective-permute-start.6 = (f32[576,512]{1,0:T(8,128)S(1)}, f32[576,512]{1,0:T(8,128)S(1)}, u32[]{:S(2)}, u32[]{:S(2)}) collective-permute-start(f32[576,512]{1,0:T(8,128)S(1)} %get-tuple-element.35), channel_id=1, source_target_pairs={{60,36},{61,37},{62,38},{63,39},{36,44},{37,45},{38,46},{39,47},{4... | collective-permute-start | bytes 3538952 | tf_op jit(solution)/shard_map/ppermute | solution.py:313
  12.1 31.0 %collective-permute-start.1 = (f32[576,512]{1,0:T(8,128)S(1)}, f32[576,512]{1,0:T(8,128)S(1)}, u32[]{:S(2)}, u32[]{:S(2)}) collective-permute-start(f32[576,512]{1,0:T(8,128)S(1)} %get-tuple-element.35), channel_id=1, source_target_pairs={{44,36},{45,37},{46,38},{47,39},{52,44},{53,45},{54,46},{55,47},{6... | collective-permute-start | bytes 3538952 | tf_op jit(solution)/shard_map/ppermute | solution.py:313
  14.2 2.0 %collective-permute-start.7 = (f32[64,512]{1,0:T(8,128)S(1)}, f32[64,512]{1,0:T(8,128)S(1)}, u32[]{:S(2)}, u32[]{:S(2)}) collective-permute-start(f32[64,512]{1,0:T(8,128)S(1)} %get-tuple-element.34.refs_2_.old_ref.vec_ref), channel_id=1, source_target_pairs={{0,4},{1,5},{2,6},{3,7},{4,12},{5,13},{6,14},{7,15},{8,0},{9,1},{1... | collective-permute-start | bytes 393224 | tf_op jit(solution)/shard_map/ppermute | solution.py:313
  14.3 19.5 %collective-permute-start.2 = (f32[192,512]{1,0:T(8,128)S(1)}, f32[192,512]{1,0:T(8,128)S(1)}, u32[]{:S(2)}, u32[]{:S(2)}) collective-permute-start(f32[192,512]{1,0:T(8,128)S(1)} %get-tuple-element.39), channel_id=1, source_target_pairs={{0,4},{1,5},{2,6},{3,7},{4,0},{5,1},{6,2},{7,3},{8,12},{9,13},{10,... | collective-permute-start | bytes 1179656 | tf_op jit(solution)/shard_map/ppermute | solution.py:313
  16.3 1.4 %collective-permute-start.8 = (f32[64,512]{1,0:T(8,128)S(1)}, f32[64,512]{1,0:T(8,128)S(1)}, u32[]{:S(2)}, u32[]{:S(2)}) collective-permute-start(f32[64,512]{1,0:T(8,128)S(1)} %get-tuple-element.49.old_ref), channel_id=1, source_target_pairs={{0,4},{1,5},{2,6},{3,7},{4,0},{5,1},{6,2},{7,3},{8,12},{9,13},{10,... | collective-permute-start | bytes 393224 | tf_op jit(solution)/shard_map/ppermute | solution.py:313
  17.7 1.4 %collective-permute-start.9 = (f32[64,512]{1,0:T(8,128)S(1)}, f32[64,512]{1,0:T(8,128)S(1)}, u32[]{:S(2)}, u32[]{:S(2)}) collective-permute-start(f32[64,512]{1,0:T(8,128)S(1)} %get-tuple-element.51.old_ref), channel_id=1, source_target_pairs={{0,4},{1,5},{2,6},{3,7},{4,0},{5,1},{6,2},{7,3},{8,12},{9,13},{10,... | collective-permute-start | bytes 393224 | tf_op jit(solution)/shard_map/ppermute | solution.py:313
  19.2 14.8 %collective-permute-start.11 = (f32[64,512]{1,0:T(8,128)S(1)}, f32[64,512]{1,0:T(8,128)S(1)}, u32[]{:S(2)}, u32[]{:S(2)}) collective-permute-start(f32[64,512]{1,0:T(8,128)S(1)} %get-tuple-element.54.walk_end_ref), channel_id=1, source_target_pairs={{0,4},{1,5},{2,6},{3,7},{4,0},{5,1},{6,2},{7,3},{8,12},{9,13},{10,... | collective-permute-start | bytes 393224 | tf_op jit(solution)/shard_map/ppermute | solution.py:313
  19.4 16.5 %collective-permute-start.10 = (f32[64,512]{1,0:T(8,128)S(1)}, f32[64,512]{1,0:T(8,128)S(1)}, u32[]{:S(2)}, u32[]{:S(2)}) collective-permute-start(f32[64,512]{1,0:T(8,128)S(1)} %get-tuple-element.54.walk_end_ref), channel_id=1, source_target_pairs={{0,4},{1,5},{2,6},{3,7},{4,0},{5,1},{6,2},{7,3},{8,12},{9,13},{10,... | collective-permute-start | bytes 393224 | tf_op jit(solution)/shard_map/ppermute | solution.py:313
  33.9 6.9 %collective-permute-start.5 = (f32[128,512]{1,0:T(8,128)S(1)}, f32[128,512]{1,0:T(8,128)S(1)}, u32[]{:S(2)}, u32[]{:S(2)}) collective-permute-start(f32[128,512]{1,0:T(8,128)S(1)} %slice.6), channel_id=1, source_target_pairs={{0,4},{1,5},{2,6},{3,7},{4,0},{5,1},{6,2},{7,3},{8,12},{9,13},{10,... | collective-permute-start | bytes 786440 | tf_op jit(solution)/shard_map/ppermute | solution.py:313
  34.0 8.7 %collective-permute-start.4 = (f32[128,512]{1,0:T(8,128)S(1)}, f32[128,512]{1,0:T(8,128)S(1)}, u32[]{:S(2)}, u32[]{:S(2)}) collective-permute-start(f32[128,512]{1,0:T(8,128)S(1)} %slice.6), channel_id=1, source_target_pairs={{0,4},{1,5},{2,6},{3,7},{4,0},{5,1},{6,2},{7,3},{8,12},{9,13},{10,... | collective-permute-start | bytes 786440 | tf_op jit(solution)/shard_map/ppermute | solution.py:313
  35.9 6.8 %collective-permute-start.3 = (f32[128,512]{1,0:T(8,128)S(1)}, f32[128,512]{1,0:T(8,128)S(1)}, u32[]{:S(2)}, u32[]{:S(2)}) collective-permute-start(f32[128,512]{1,0:T(8,128)S(1)} %slice.6), channel_id=1, source_target_pairs={{0,4},{1,5},{2,6},{3,7},{4,0},{5,1},{6,2},{7,3},{8,12},{9,13},{10,... | collective-permute-start | bytes 786440 | tf_op jit(solution)/shard_map/ppermute | solution.py:313
  40.8 2.5 %collective-permute-start.12 = (f32[64,512]{1,0:T(8,128)S(1)}, f32[64,512]{1,0:T(8,128)S(1)}, u32[]{:S(2)}, u32[]{:S(2)}) collective-permute-start(f32[64,512]{1,0:T(8,128)S(1)} %shard_map.55.refs_12_), channel_id=1, source_target_pairs={{0,4},{1,5},{2,6},{3,7},{4,0},{5,1},{6,2},{7,3},{8,12},{9,13},{10,... | collective-permute-start | bytes 393224 | tf_op jit(solution)/shard_map/ppermute | solution.py:313
  43.5 1.4 %collective-permute-start.13 = (f32[64,512]{1,0:T(8,128)S(1)}, f32[64,512]{1,0:T(8,128)S(1)}, u32[]{:S(2)}, u32[]{:S(2)}) collective-permute-start(f32[64,512]{1,0:T(8,128)S(1)} %get-tuple-element.56), channel_id=1, source_target_pairs={{0,4},{1,5},{2,6},{3,7},{4,0},{5,1},{6,2},{7,3},{8,12},{9,13},{10,... | collective-permute-start | bytes 393224 | tf_op jit(solution)/shard_map/ppermute | solution.py:313
  45.0 7.1 %collective-permute-start.14 = (f32[64,512]{1,0:T(8,128)S(1)}, f32[64,512]{1,0:T(8,128)S(1)}, u32[]{:S(2)}, u32[]{:S(2)}) collective-permute-start(f32[64,512]{1,0:T(8,128)S(1)} %get-tuple-element.58), channel_id=1, source_target_pairs={{0,4},{1,5},{2,6},{3,7},{4,0},{5,1},{6,2},{7,3},{8,12},{9,13},{10,... | collective-permute-start | bytes 393224 | tf_op jit(solution)/shard_map/ppermute | solution.py:313
  52.5 1.4 %collective-permute-start.15 = (f32[64,512]{1,0:T(8,128)S(1)}, f32[64,512]{1,0:T(8,128)S(1)}, u32[]{:S(2)}, u32[]{:S(2)}) collective-permute-start(f32[64,512]{1,0:T(8,128)S(1)} %shard_map.59.in_ref), channel_id=1, source_target_pairs={{0,4},{4,0},{1,5},{5,1},{2,6},{6,2},{3,7},{7,3},{8,12},{12,8},{9,1... | collective-permute-start | bytes 393224 | tf_op jit(solution)/shard_map/ppermute | solution.py:355
